TPU v7x, 128 devices: a whole 4x4x4 slice. The times are simulated.
128 devices in a mesh: rep: 16 (over y, x_hi, core), tp: 8 (over x_lo, z).
Axes of the slice: x: 4 (x_hi: 2, x_lo: 2; x = x_hi * 2 + x_lo), y: 4, z: 4, core: 2. Of those that a mesh axis runs over, the one named last changes fastest.
Arguments:
- hidden: bfloat16 [1024, 8192], P('rep'), may hold values from -6 to 6
- norm_gain: bfloat16 [8192], replicated, may hold values from 0.5 to 1.5
- query_weight_matrix: bfloat16 [8192, 4096], P(None, 'tp'), may hold values from -0.0625 to 0.0625
- key_value_weight: bfloat16 [2, 8192, 1024], P(None, None, 'tp'), may hold values from -0.0625 to 0.0625
- output_weight_matrix: bfloat16 [4096, 8192], P('tp'), may hold values from -0.375 to 0.375
- input_down_factors: bfloat16 [3, 8192, 64], P(None, ('rep', 'tp')), may hold values from -0.0625 to 0.0625
- query_up_factor: bfloat16 [64, 4096], P(None, ('rep', 'tp')), may hold values from -0.75 to 0.75
- key_value_up_factors: bfloat16 [2, 64, 1024], P(None, None, ('rep', 'tp')), may hold values from -0.75 to 0.75
- output_down_factor: bfloat16 [4096, 64], P(('rep', 'tp')), may hold values from -0.375 to 0.375
- output_up_factor: bfloat16 [64, 8192], P(None, ('rep', 'tp')), may hold values from -0.75 to 0.75
- cache_keys: bfloat16 [1024, 8, 128, 128], P('rep', 'tp'), may hold values from -360 to 360
- cache_values: bfloat16 [1024, 8, 128, 128], P('rep', 'tp'), may hold values from -6 to 6
- lengths: int32 [1024], P('rep'), may hold values from 1 to 127
Outputs:
- attn_out: bfloat16 [1024, 8192], P('rep', 'tp')
All inputs are finite; a program needn't handle non-finite values.
Results may differ from a plain program's by a relative error of at most 0.03.
Values may be sent and summed in bfloat16 or wider, within the bound.
A program may use at most 128 MiB of HBM per device.

v0:
```python
import math

import jax
import jax.numpy as jnp
from jax import lax
from jax.sharding import Mesh
from jax.sharding import PartitionSpec as P

REP = ("rep_0", "rep_1", "rep_2")
REP_TP = ("rep_0", "rep_1", "rep_2", "tp")


epsilon = 1e-06
rope_base = 1000000.0
adapter_scale = 0.5


def joined_along(parts, dim):
    parts = jnp.moveaxis(parts, 0, dim)
    dims = parts.shape
    return parts.reshape(*dims[:dim], dims[dim] * dims[dim + 1], *dims[dim + 2 :])


def gather_in_order(array, axes, order):
    parts = array
    for k in order:
        parts = lax.all_gather(parts, axes[k])
    done = order[::-1]
    back = [done.index(k) for k in range(len(axes))]
    parts = parts.transpose(*back, *range(len(axes), parts.ndim))
    return parts.reshape(-1, *array.shape)


def gather_axes(array, axes, order, dim):
    return joined_along(gather_in_order(array, axes, order), dim)


def from_everyone(array, axis):
    count = lax.axis_size(axis)
    return lax.all_to_all(
        jnp.broadcast_to(array[None], (count, *array.shape)), axis, 0, 0, tiled=True
    )


def of_everyone(array, axis):
    return from_everyone(array, axis).astype(jnp.float32).sum(axis=0)


def one_gather(arrays, axis, dims):
    line = jnp.concatenate([a.reshape(-1) for a in arrays])
    lines, at, done = (lax.all_gather(line, axis), 0, [])
    for a, dim in zip(arrays, dims):
        parts = lines[:, at : at + a.size].reshape(-1, *a.shape)
        done.append(joined_along(parts, dim))
        at += a.size
    return tuple(done)


def in_one_piece(arrays, axis, split_dim, concat_dim, along):
    ends, at = ([], 0)
    for a in arrays[:-1]:
        at += a.shape[along]
        ends.append(at)
    both = jnp.concatenate(arrays, axis=along)
    return tuple(
        jnp.split(
            lax.all_to_all(both, axis, split_axis=split_dim, concat_axis=concat_dim, tiled=True),
            ends,
            axis=along,
        )
    )


def over_copies(array, axis):
    everything = from_everyone(array, axis)
    return jnp.sum(everything, axis=0)


def in_blocks(array, dim, count):
    dims = array.shape
    parts = array.reshape(*dims[:dim], count, dims[dim] // count, *dims[dim + 1 :])
    return jnp.moveaxis(parts, dim, 0)


def sum_at_owner(array, axis, dim):
    parts = in_blocks(array, dim, lax.axis_size(axis))
    arrived = lax.all_to_all(parts, axis, split_axis=0, concat_axis=0, tiled=True)
    return arrived.astype(jnp.float32).sum(axis=0)


def rope_angles(lengths, head_dim):
    half_dim = head_dim // 2
    frequency = rope_base ** (-(jnp.arange(half_dim, dtype=jnp.float32) * 2.0) / head_dim)
    return lengths.astype(jnp.float32)[:, None] * frequency[None, :]


def rotate(vectors, angles):
    half_dim = vectors.shape[-1] // 2
    cosine = jnp.cos(angles)[:, None, :]
    sine_part = jnp.sin(angles)[:, None, :]
    low_half = vectors[..., :half_dim]
    high_half = vectors[..., half_dim:]
    return jnp.concatenate(
        [low_half * cosine - high_half * sine_part, high_half * cosine + low_half * sine_part],
        axis=-1,
    )


def adapted(normed, frozen_matrix, inner_part, up_factor):
    base_part = jnp.dot(normed, frozen_matrix, preferred_element_type=jnp.float32)
    return base_part + adapter_scale * jnp.dot(
        inner_part, up_factor, preferred_element_type=jnp.float32
    )


def attend(query, new_key, new_value, keys, values, lengths):
    score_scale = 1.0 / math.sqrt(keys.shape[-1])
    scores = jnp.einsum("bkgd,bkld->bkgl", query, keys.astype(jnp.float32)) * score_scale
    own_score = jnp.sum(query * new_key.astype(jnp.float32)[:, :, None, :], axis=-1) * score_scale
    live_mask = (
        jnp.arange(keys.shape[2], dtype=jnp.int32)[None, None, None, :]
        < lengths[:, None, None, None]
    )
    row_max = jnp.maximum(jnp.max(jnp.where(live_mask, scores, -1e30), axis=-1), own_score)
    weights = jnp.where(live_mask, jnp.exp(scores - row_max[..., None]), 0.0)
    own_weight = jnp.exp(own_score - row_max)
    denom_sum = jnp.sum(weights, axis=-1) + own_weight
    probs = (weights / denom_sum[..., None]).astype(jnp.bfloat16)
    own_prob = (own_weight / denom_sum).astype(jnp.bfloat16)
    context = jnp.einsum("bkgl,bkld->bkgd", probs, values, preferred_element_type=jnp.float32)
    context = (
        context
        + own_prob.astype(jnp.float32)[..., None] * new_value.astype(jnp.float32)[:, :, None, :]
    )
    return context.astype(jnp.bfloat16)


def regroup(factor, tp_count, group):
    count, rank_dim, wide = factor.shape
    return factor.reshape(count, rank_dim, tp_count, group, wide // (tp_count * group))


def settle(factor):
    count, rank_dim, tp_count, group, piece = factor.shape
    return jnp.swapaxes(factor, 2, 3).reshape(count, rank_dim, group * tp_count * piece)


def local(
    hidden,
    norm_gain,
    query_weight_matrix,
    key_value_weight,
    output_weight_matrix,
    input_down_factors,
    query_up_factor,
    key_value_up_factors,
    output_down_factor,
    output_up_factor,
    cache_keys,
    cache_values,
    lengths,
):
    states = hidden.astype(jnp.float32)
    square = jnp.mean(states * states, axis=-1, keepdims=True)
    normed = (states * lax.rsqrt(square + epsilon) * norm_gain.astype(jnp.float32)).astype(
        jnp.bfloat16
    )
    seq_count = hidden.shape[0]
    block_rows = input_down_factors.shape[1]
    rep_count = lax.axis_size(REP)
    tp_count = lax.axis_size("tp")
    tp_index = lax.axis_index("tp")
    own_features = lax.dynamic_slice_in_dim(
        normed.reshape(seq_count, rep_count, tp_count, block_rows), tp_index, 1, 2
    )
    own_features = own_features.reshape(seq_count, rep_count * block_rows)
    partial_inner = jnp.einsum(
        "bd,jdr->jbr",
        own_features,
        gather_axes(input_down_factors, REP, (1, 0, 2), 1),
        preferred_element_type=jnp.float32,
    )
    inner = (
        of_everyone(partial_inner.astype(jnp.bfloat16), "tp")
        .astype(jnp.float32)
        .astype(jnp.bfloat16)
    )
    query_up_rows = query_up_factor[None]
    out_down_rows = jnp.swapaxes(output_down_factor, 0, 1)[None]
    out_up_rows = output_up_factor[None]
    per_rep = one_gather(
        (query_up_rows, key_value_up_factors, out_down_rows, out_up_rows), REP, (2, 2, 2, 2)
    )
    group = rep_count // tp_count
    arrived = (
        lax.all_to_all(
            regroup(per_rep[0], tp_count, group), "tp", split_axis=2, concat_axis=2, tiled=True
        ),
        lax.all_to_all(
            regroup(per_rep[1], tp_count, group), "tp", split_axis=2, concat_axis=2, tiled=True
        ),
        *in_one_piece(
            (regroup(per_rep[2], tp_count, group), regroup(per_rep[3], tp_count, group)),
            "tp",
            2,
            2,
            4,
        ),
    )
    query_up_local = settle(arrived[0])
    key_value_up_local = settle(arrived[1])
    out_down_local = settle(arrived[2])
    out_up_local = settle(arrived[3])
    kv_local = cache_keys.shape[1]
    head_dim = cache_keys.shape[3]
    angles = rope_angles(lengths, head_dim)
    query = adapted(normed, query_weight_matrix, inner[0], query_up_local[0]).reshape(
        seq_count, -1, head_dim
    )
    query = rotate(query, angles).reshape(seq_count, kv_local, -1, head_dim)
    new_key = adapted(normed, key_value_weight[0], inner[1], key_value_up_local[0]).reshape(
        seq_count, kv_local, head_dim
    )
    new_key = rotate(new_key, angles).astype(jnp.bfloat16)
    new_value = (
        adapted(normed, key_value_weight[1], inner[2], key_value_up_local[1])
        .reshape(seq_count, kv_local, head_dim)
        .astype(jnp.bfloat16)
    )
    context = attend(query, new_key, new_value, cache_keys, cache_values, lengths).reshape(
        seq_count, -1
    )
    partial_middle = jnp.einsum(
        "bh,rh->br", context, out_down_local[0], preferred_element_type=jnp.float32
    )
    middle = over_copies(partial_middle, "tp").astype(jnp.bfloat16)
    partial_value = jnp.dot(context, output_weight_matrix, preferred_element_type=jnp.float32)
    summed = sum_at_owner(partial_value.astype(jnp.bfloat16), "tp", 1)
    summed = summed + adapter_scale * jnp.dot(
        middle, out_up_local[0], preferred_element_type=jnp.float32
    )
    return summed.astype(jnp.bfloat16)


def solution(mesh):
    finer = Mesh(mesh.devices.reshape(4, 2, 2, mesh.shape["tp"]), ("rep_0", "rep_1", "rep_2", "tp"))
    placed = (
        P(REP, None),
        P(),
        P(None, "tp"),
        P(None, None, "tp"),
        P("tp", None),
        P(None, REP_TP, None),
        P(None, REP_TP),
        P(None, None, REP_TP),
        P(REP_TP, None),
        P(None, REP_TP),
        P(REP, "tp", None, None),
        P(REP, "tp", None, None),
        P(REP),
    )
    return jax.shard_map(
        local, mesh=finer, in_specs=placed, out_specs=P(REP, "tp"), check_vma=False
    )
```

profile of v0, /device:TPU:0, one launch (start us, length us, event | category | flops | bytes accessed | tf_op | source)
XLA Modules:
  0.0 182.1 jit_solution(5192727470760540867)
XLA Ops:
  3.6 27.1 %all-gather.3 = bf16[147456]{0:T(1024)(128)(2,1)} all-gather(bf16[9216]{0:T(1024)(128)(2,1)S(1)} %pad_maximum_fusion), channel_id=5, replica_groups=mesh['rep_0'=4,'rep_1'=2,'rep_2'=2,'tp'=8] {'rep_0','rep_1','rep_2'}, dimensions={0}, use_global_device_ids=true | all-gather | bytes 313344 | tf_op jit(solution)/shard_map/all_gather | solution.py:51
  36.0 5.3 %all-to-all-start.2 = ((bf16[8,2,1024]{2,1,0:T(2,128)(2,1)}), bf16[8,2,1024]{2,1,0:T(2,128)(2,1)}, u32[]{:S(2)}, u32[]{:S(2)}) async-start(bf16[8,2,1024]{2,1,0:T(2,128)(2,1)} %reshape.346), calls=%async_computation.2 | async-start | bytes 65536 | tf_op jit(solution)/shard_map/all_to_all | solution.py:199
  44.7 3.3 %reshape.319 = bf16[64,16,8,64]{3,2,1,0:T(8,128)(2,1)} reshape(bf16[64,8192]{1,0:T(8,128)(2,1)S(1)} %fusion.2) | data formatting | bytes 2097152 | tf_op jit(solution)/shard_map/reshape | solution.py:174
  48.0 3.3 %dynamic-slice_reduce_fusion = bf16[64,16,64]{2,1,0:T(8,128)(2,1)S(1)} fusion(bf16[64,16,8,64]{3,2,1,0:T(8,128)(2,1)} %reshape.319, s32[]{:T(128)S(6)} %select_n.12), kind=kLoop, calls=%fused_computation.35 | loop fusion | bytes 262148 | tf_op jit(solution)/shard_map/dynamic_slice | solution.py:173
  52.1 6.2 %all-gather = bf16[6,64,64]{2,1,0:T(8,128)(2,1)S(1)} all-gather(bf16[3,64,64]{2,1,0:T(8,128)(2,1)S(1)} %copy-done.10), channel_id=2, replica_groups=mesh['rep_0'=4,'rep_1'=2,'rep_2'=2,'tp'=8] {'rep_1'}, dimensions={0}, use_global_device_ids=true | all-gather | bytes 73728 | tf_op jit(solution)/shard_map/all_gather | solution.py:27
  58.4 12.5 %all-gather.1 = bf16[8,3,64,64]{3,2,1,0:T(8,128)(2,1)S(1)} all-gather(bf16[2,3,64,64]{3,2,1,0:T(8,128)(2,1)S(1)} %bitcast.141), channel_id=3, replica_groups=mesh['rep_0'=4,'rep_1'=2,'rep_2'=2,'tp'=8] {'rep_0'}, dimensions={0}, use_global_device_ids=true | all-gather | bytes 245760 | tf_op jit(solution)/shard_map/all_gather | solution.py:27
  70.9 2.4 %all-gather.2 = bf16[8,2,3,64,64]{4,3,2,1,0:T(8,128)(2,1)S(1)} all-gather(bf16[4,2,3,64,64]{4,3,2,1,0:T(8,128)(2,1)S(1)} %bitcast.129), channel_id=4, replica_groups=mesh['rep_0'=4,'rep_1'=2,'rep_2'=2,'tp'=8] {'rep_2'}, dimensions={0}, use_global_device_ids=true | all-gather | bytes 589824 | tf_op jit(solution)/shard_map/all_gather | solution.py:27
  74.2 2.6 %copy.93 = bf16[3,16,64,64]{2,1,3,0:T(8,128)(2,1)} copy(bf16[3,16,64,64]{3,2,0,1:T(8,128)(2,1)} %bitcast.128) | data formatting | bytes 786432 | tf_op jit(solution)/shard_map/transpose | solution.py:19
  78.6 5.6 %fusion.72 = f32[64,512]{1,0:T(8,128)} fusion(bf16[64,8192]{1,0:T(8,128)(2,1)S(1)} %fusion.2, bf16[8192,512]{1,0:T(8,128)(2,1)} %param.15), kind=kOutput, calls=%fused_computation.94 | convolution fusion | flops 536870912 | bytes 9568256 | tf_op jit(solution)/shard_map/dot_general | solution.py:110
  85.9 1.9 %reshape.333 = bf16[16,1,64,64]{3,2,0,1:T(8,128)(2,1)} reshape(bf16[16,4096]{1,0:T(8,128)(2,1)} %slice.74) | data formatting | bytes 262144 | tf_op jit(solution)/shard_map/reshape | solution.py:53
  94.8 5.7 %all-to-all-start.1 = ((bf16[8,2,2048]{2,1,0:T(2,128)(2,1)}), bf16[8,2,2048]{2,1,0:T(2,128)(2,1)S(1)}, u32[]{:S(2)}, u32[]{:S(2)}) async-start(bf16[8,2,2048]{2,1,0:T(2,128)(2,1)} %reshape.342), calls=%async_computation.1 | async-start | bytes 131072 | tf_op jit(solution)/shard_map/all_to_all | solution.py:196
  102.7 4.2 %all-to-all-done.1 = bf16[8,2,2048]{2,1,0:T(2,128)(2,1)S(1)} async-done(((bf16[8,2,2048]{2,1,0:T(2,128)(2,1)}), bf16[8,2,2048]{2,1,0:T(2,128)(2,1)S(1)}, u32[]{:S(2)}, u32[]{:S(2)}) %all-to-all-start.1) | async-done | bytes 65568 | tf_op jit(solution)/shard_map/all_to_all | solution.py:196
  106.9 3.4 %all-to-all-start = ((bf16[8,2,6144]{2,1,0:T(2,128)(2,1)}), bf16[8,2,6144]{2,1,0:T(2,128)(2,1)S(1)}, u32[]{:S(2)}, u32[]{:S(2)}) async-start(bf16[8,2,6144]{2,1,0:T(2,128)(2,1)} %reshape.344), calls=%async_computation | async-start | bytes 393216 | tf_op jit(solution)/shard_map/all_to_all | solution.py:40
  111.1 6.0 %all-to-all-done = bf16[8,2,6144]{2,1,0:T(2,128)(2,1)S(1)} async-done(((bf16[8,2,6144]{2,1,0:T(2,128)(2,1)}), bf16[8,2,6144]{2,1,0:T(2,128)(2,1)S(1)}, u32[]{:S(2)}, u32[]{:S(2)}) %all-to-all-start) | async-done | bytes 196640 | tf_op jit(solution)/shard_map/all_to_all | solution.py:40
  117.8 3.6 %all-to-all-start.4 = ((bf16[1,64,8,2,96]{4,1,3,0,2:T(8,128)(2,1)}), bf16[1,64,8,2,96]{4,1,3,0,2:T(8,128)(2,1)S(1)}, u32[]{:S(2)}, u32[]{:S(2)}) async-start(bf16[1,64,8,2,96]{4,1,3,0,2:T(8,128)(2,1)} %maximum_bitcast_fusion), calls=%async_computation.4 | async-start | bytes 524288 | tf_op jit(solution)/shard_map/all_to_all | solution.py:67
  121.4 2.0 %reshape.345 = bf16[8,3,64,64]{3,2,1,0:T(8,128)(2,1)} reshape(bf16[8,2,6144]{2,1,0:T(2,128)(2,1)} %copy-done.3) | data formatting | bytes 393216
  126.1 2.1 %fusion.29 = f32[64,1,128]{2,0,1:T(8,128)S(1)} fusion(f32[64,128]{1,0:T(8,128)S(1)} %convolution_multiply_fusion.3, bf16[64,8192]{1,0:T(8,128)(2,1)S(1)} %fusion.2, bf16[2,8192,128]{2,1,0:T(8,128)(2,1)} %param.16), kind=kOutput, calls=%fused_computation.28 | convolution fusion | flops 134225920 | bytes 3211264 | tf_op jit(solution)/shard_map/dot_general | solution.py:110
  136.4 3.4 %select_reduce_fusion = (f32[64,4]{1,0:T(8,128)}, f32[64,4,128]{2,1,0:T(4,128)}) fusion(pred[64,128]{1,0:T(8,128)(4,1)S(1)} %iota_compare_fusion, bf16[64,1,128,128]{3,2,1,0:T(8,128)(2,1)S(1)} %copy-done, f32[64,4,64]{2,1,0:T(4,128)} %copy-done.2, f32[64,4,64]{2,1,0:T(4,128)S(1)} %get-tuple-element.7), kind=kOutput, calls=%fused_computation.45 | convolution fusion | flops 8617728 | bytes 2368512 | tf_op jit(solution)/shard_map/bkgd,bkld->bkgl/dot_general | solution.py:118
  144.3 2.7 %fusion.38 = f32[64,128]{1,0:T(8,128)} fusion(f32[64,128]{1,0:T(8,128)S(1)} %convolution_multiply_fusion.2, bf16[64,8192]{1,0:T(8,128)(2,1)S(1)} %fusion.2, bf16[2,8192,128]{2,1,0:T(8,128)(2,1)} %param.16), kind=kOutput, calls=%fused_computation.33 | convolution fusion | flops 134242304 | bytes 3211264 | tf_op jit(solution)/shard_map/dot_general | solution.py:110
  147.3 2.4 %fusion.22 = bf16[64,4,128]{2,1,0:T(4,128)(2,1)S(1)} fusion(bf16[64,1,128,128]{3,2,1,0:T(8,128)(2,1)} %param.24, f32[64,4,128]{2,1,0:T(4,128)S(1)} %copy-done.5, f32[64,128]{1,0:T(8,128)} %fusion.38, f32[64,4]{1,0:T(8,128)} %copy.108, f32[64,4]{1,0:T(8,128)} %copy.107, f32[64,4]{1,0:T(8,128)} %copy-done.9, pred[64,128]{1,0:T(8,128)(4,1)S(1)} %iota_compare_fusion), kind=kOutput, calls=%fused_computation.24 | convolution fusion | flops 8617984 | bytes 2337792 | tf_op jit(solution)/shard_map/bkgl,bkld->bkgd/dot_general | solution.py:130
  151.3 5.4 %all-to-all-start.5 = ((f32[8,1,4096]{2,1,0:T(1,128)}), f32[8,1,4096]{2,1,0:T(1,128)S(1)}, u32[]{:S(2)}, u32[]{:S(2)}) async-start(f32[8,1,4096]{2,1,0:T(1,128)} %reshape.348), calls=%async_computation.5 | async-start | bytes 262144 | tf_op jit(solution)/shard_map/all_to_all | solution.py:40
  156.7 5.0 %convolution_convert_fusion = bf16[64,8192]{1,0:T(8,128)(2,1)S(1)} fusion(bf16[512,8192]{1,0:T(8,128)(2,1)} %param.17, bf16[8,8,4,128]{3,2,1,0:T(4,128)(2,1)} %bitcast.140), kind=kOutput, calls=%fused_computation | convolution fusion | flops 537395200 | bytes 9502720 | tf_op jit(solution)/shard_map/dot_general | solution.py:237
  163.3 5.2 %all-to-all-start.3 = ((bf16[8,64,1024]{2,1,0:T(8,128)(2,1)}), bf16[8,64,1024]{2,1,0:T(8,128)(2,1)S(1)}, u32[]{:S(2)}, u32[]{:S(2)}) async-start(bf16[8,64,1024]{2,1,0:T(8,128)(2,1)} %bitcast.125), calls=%async_computation.3 | async-start | bytes 2097152 | tf_op jit(solution)/shard_map/all_to_all | solution.py:87
  172.1 8.1 %all-to-all-done.3 = bf16[8,64,1024]{2,1,0:T(8,128)(2,1)S(1)} async-done(((bf16[8,64,1024]{2,1,0:T(8,128)(2,1)}), bf16[8,64,1024]{2,1,0:T(8,128)(2,1)S(1)}, u32[]{:S(2)}, u32[]{:S(2)}) %all-to-all-start.3) | async-done | bytes 1048608 | tf_op jit(solution)/shard_map/all_to_all | solution.py:87
  (105 shorter events, 52.3 us)
Async XLA Ops:
  0.0 136.4 %copy-start = (bf16[64,1,128,128]{3,2,1,0:T(8,128)(2,1)S(1)}, bf16[64,1,128,128]{3,2,1,0:T(8,128)(2,1)}, u32[]{:S(2)}) copy-start(bf16[64,1,128,128]{3,2,1,0:T(8,128)(2,1)} %param.23) | copy-start | bytes 6291460
  0.0 42.0 %copy-start.12 = (s32[64]{0:T(128)S(1)}, s32[64]{0:T(128)}, u32[]{:S(2)}) copy-start(s32[64]{0:T(128)} %param.25) | copy-start | bytes 772
  0.0 42.8 %copy-start.11 = (bf16[8192]{0:T(1024)(128)(2,1)S(1)}, bf16[8192]{0:T(1024)(128)(2,1)}, u32[]{:S(2)}) copy-start(bf16[8192]{0:T(1024)(128)(2,1)} %param.14) | copy-start | bytes 49156
  0.0 42.8 %copy-start.1 = (bf16[64,8192]{1,0:T(8,128)(2,1)S(1)}, bf16[64,8192]{1,0:T(8,128)(2,1)}, u32[]{:S(2)}) copy-start(bf16[64,8192]{1,0:T(8,128)(2,1)} %param.13) | copy-start | bytes 3145732
  36.0 58.8 %all-to-all-start.2 = ((bf16[8,2,1024]{2,1,0:T(2,128)(2,1)}), bf16[8,2,1024]{2,1,0:T(2,128)(2,1)}, u32[]{:S(2)}, u32[]{:S(2)}) async-start(bf16[8,2,1024]{2,1,0:T(2,128)(2,1)} %reshape.346), calls=%async_computation.2 | async-start | bytes 65536 | tf_op jit(solution)/shard_map/all_to_all | solution.py:199
  44.7 7.5 %copy-start.10 = (bf16[3,64,64]{2,1,0:T(8,128)(2,1)S(1)}, bf16[3,64,64]{2,1,0:T(8,128)(2,1)}, u32[]{:S(2)}) copy-start(bf16[3,64,64]{2,1,0:T(8,128)(2,1)} %param.18) | copy-start | bytes 73732
  94.8 12.1 %all-to-all-start.1 = ((bf16[8,2,2048]{2,1,0:T(2,128)(2,1)}), bf16[8,2,2048]{2,1,0:T(2,128)(2,1)S(1)}, u32[]{:S(2)}, u32[]{:S(2)}) async-start(bf16[8,2,2048]{2,1,0:T(2,128)(2,1)} %reshape.342), calls=%async_computation.1 | async-start | bytes 131072 | tf_op jit(solution)/shard_map/all_to_all | solution.py:196
  106.9 10.3 %all-to-all-start = ((bf16[8,2,6144]{2,1,0:T(2,128)(2,1)}), bf16[8,2,6144]{2,1,0:T(2,128)(2,1)S(1)}, u32[]{:S(2)}, u32[]{:S(2)}) async-start(bf16[8,2,6144]{2,1,0:T(2,128)(2,1)} %reshape.344), calls=%async_computation | async-start | bytes 393216 | tf_op jit(solution)/shard_map/all_to_all | solution.py:40
  117.2 0.7 copy-start.3
  117.8 29.2 %all-to-all-start.4 = ((bf16[1,64,8,2,96]{4,1,3,0,2:T(8,128)(2,1)}), bf16[1,64,8,2,96]{4,1,3,0,2:T(8,128)(2,1)S(1)}, u32[]{:S(2)}, u32[]{:S(2)}) async-start(bf16[1,64,8,2,96]{4,1,3,0,2:T(8,128)(2,1)} %maximum_bitcast_fusion), calls=%async_computation.4 | async-start | bytes 524288 | tf_op jit(solution)/shard_map/all_to_all | solution.py:67
  121.4 7.6 %copy-start.4 = (f32[64,512]{1,0:T(8,128)S(1)}, f32[64,512]{1,0:T(8,128)}, u32[]{:S(2)}) copy-start(f32[64,512]{1,0:T(8,128)} %fusion.72) | copy-start | bytes 393220
  125.1 3.9 %copy-start.6 = (bf16[1,64,2,8,32]{1,4,3,2,0:T(8,128)(2,1)S(1)}, bf16[1,64,2,8,32]{1,4,3,2,0:T(8,128)(2,1)}, u32[]{:S(2)}) copy-start(bf16[1,64,2,8,32]{1,4,3,2,0:T(8,128)(2,1)} %copy.98) | copy-start | bytes 196612
  134.1 0.7 copy-start.2
  140.7 2.7 %copy-start.9 = (f32[64,4]{1,0:T(8,128)}, f32[64,4]{1,0:T(8,128)S(1)}, u32[]{:S(2)}) copy-start(f32[64,4]{1,0:T(8,128)S(1)} %copy.105) | copy-start | bytes 3076
  143.4 3.9 %copy-start.5 = (f32[64,4,128]{2,1,0:T(4,128)S(1)}, f32[64,4,128]{2,1,0:T(4,128)}, u32[]{:S(2)}) copy-start(f32[64,4,128]{2,1,0:T(4,128)} %get-tuple-element.18) | copy-start | bytes 393220
  149.6 0.6 copy-start.8
  151.3 12.0 %all-to-all-start.5 = ((f32[8,1,4096]{2,1,0:T(1,128)}), f32[8,1,4096]{2,1,0:T(1,128)S(1)}, u32[]{:S(2)}, u32[]{:S(2)}) async-start(f32[8,1,4096]{2,1,0:T(1,128)} %reshape.348), calls=%async_computation.5 | async-start | bytes 262144 | tf_op jit(solution)/shard_map/all_to_all | solution.py:40
  163.3 6.4 %copy-start.7 = (f32[8,1,4096]{2,1,0:T(1,128)}, f32[8,1,4096]{2,1,0:T(1,128)S(1)}, u32[]{:S(2)}) copy-start(f32[8,1,4096]{2,1,0:T(1,128)S(1)} %all-to-all-done.5) | copy-start | bytes 393220
  163.3 16.9 %all-to-all-start.3 = ((bf16[8,64,1024]{2,1,0:T(8,128)(2,1)}), bf16[8,64,1024]{2,1,0:T(8,128)(2,1)S(1)}, u32[]{:S(2)}, u32[]{:S(2)}) async-start(bf16[8,64,1024]{2,1,0:T(8,128)(2,1)} %bitcast.125), calls=%async_computation.3 | async-start | bytes 2097152 | tf_op jit(solution)/shard_map/all_to_all | solution.py:87
where the time goes:
time: 184 us; the launch traced here: 182 us
  blocking collectives  48.2 us (26%)
  local copies, waits for them, and re-layouts  45.3 us (25%)
  starting transfers between devices  28.7 us (16%)
  matrix products  27.7 us (15%)
  waiting for transfers between devices  18.9 us (10%)
  other arithmetic  13.1 us (7%)
    all_gather x1, blocking collectives, one_gather(): lines, at, done = (lax.all_gather(line, axis), 0, [])  27.1 us
    all_gather x3, blocking collectives, gather_in_order(): parts = lax.all_gather(parts, axes[k])  21.1 us
    unnamed x36, local copies, waits for them, and re-layouts  11 us
    dot_general x3, matrix products, adapted(): jnp.dot(normed, frozen_matrix, preferred_element_type=jnp.float32)  10.4 us
    all_to_all x2, starting transfers between devices, from_everyone(): lax.all_to_all(jnp.broadcast_to(array[None], (count, *array.shape)), axis...  8.84 us
    all_to_all x1, waiting for transfers between devices, sum_at_owner(): lax.all_to_all(parts, axis, split_axis=0, concat_axis=0, tiled=True)  8.09 us
    all_to_all x2, waiting for transfers between devices, from_everyone(): lax.all_to_all(jnp.broadcast_to(array[None], (count, *array.shape)), axis...  6.56 us
    all_to_all x1, starting transfers between devices, local(): lax.all_to_all(regroup(per_rep[0], tp_count, group), 'tp', split_axis=2,...  5.7 us
  transfers between devices with their start and end apart: 6, of which 4 were waited for; matrix products, arithmetic and copies ran while one was open for 38% of the time, Pallas kernels for 0%

commit v1 on v0

v1 whole, which is shorter than its diff:
```python
import math

import jax
import jax.numpy as jnp
from jax import lax
from jax.experimental import pallas as pl
from jax.experimental.pallas import tpu as pltpu
from jax.sharding import PartitionSpec as P

MESH = pl.DeviceIdType.MESH
bf16, f32 = jnp.bfloat16, jnp.float32

epsilon = 1e-06
rope_base = 1000000.0
adapter_scale = 0.5

FEATURES = 8192
SEQS = 64
RANK = 64
HEAD = 128
QCOLS = 512
OUTC = 1024
TP = 8
CHIPS = 8
CHUNKS = 8
CHUNK = FEATURES // CHUNKS
DROWS = 96
UROWS = 80
GROUP = 8


def dot(a, b):
    return jnp.dot(a, b, preferred_element_type=f32)


def dot_nt(a, b):
    return lax.dot_general(a, b, (((1,), (1,)), ((), ())), preferred_element_type=f32)


def dot_tn(a, b):
    return lax.dot_general(a, b, (((0,), (0,)), ((), ())), preferred_element_type=f32)


def at_lanes(offset, rows):
    row = lax.broadcasted_iota(jnp.int32, (rows, 128), 0)
    lane = lax.broadcasted_iota(jnp.int32, (rows, 128), 1)
    return jnp.where(lane == row + offset, 1.0, 0.0).astype(bf16)


def kernel(
    hidden, gain, wq, wkv, wo, down, qup, kvup, odown, oup, keys, values, lengths,
    out,
    hid_v, nrm_v, wq_v, wkv_v, wo_v, k_v, v_v,
    down_v, qup_v, kvup_v, odown_v, oup_v,
    dg, w2, ug, ut, inner_p, ou_v, mid_p, rs_send, rs_recv,
    qacc, kacc, vacc, q_s, own_s, ctx_s, len_s, ctx_b, out_v,
    load_sem, wq_sem, wkv_sem, small_sem,
    d_send, d_recv, dd_sem, u_send, u_recv, t_send, t_recv, tt_sem,
    i_send, i_recv, m_send, m_recv, r_send, r_recv,
):
    rep = lax.axis_index("rep")
    t = lax.axis_index("tp")
    chip = rep // 2
    core = rep % 2
    partner = chip * 2 + (1 - core)

    def chip_at(j):
        return lax.rem(chip + j, CHIPS)

    def tp_at(j):
        return lax.rem(t + j, TP)

    barrier = pltpu.get_barrier_semaphore()
    pl.semaphore_signal(barrier, inc=1, device_id=(partner, t), device_id_type=MESH)
    for j in range(1, CHIPS):
        pl.semaphore_signal(barrier, inc=1, device_id=(chip_at(j) * 2 + core, t), device_id_type=MESH)
    for j in range(1, TP):
        pl.semaphore_signal(barrier, inc=1, device_id=(rep, tp_at(j)), device_id_type=MESH)

    small = [
        pltpu.make_async_copy(src, dst, small_sem.at[i])
        for i, (src, dst) in enumerate(
            ((down, down_v), (qup, qup_v), (kvup, kvup_v), (odown, odown_v), (oup, oup_v))
        )
    ]
    for copy in small:
        copy.start()
    hid_copy = pltpu.make_async_copy(hidden, hid_v, load_sem.at[0])
    hid_copy.start()

    def wq_copy(i):
        rows = pl.ds(pl.multiple_of(i * CHUNK, CHUNK), CHUNK)
        return pltpu.make_async_copy(wq.at[rows, :], wq_v.at[rows, :], wq_sem.at[i])

    def wkv_copy(i):
        rows = pl.ds(pl.multiple_of(i * CHUNK, CHUNK), CHUNK)
        return pltpu.make_async_copy(wkv.at[:, rows, :], wkv_v.at[:, rows, :], wkv_sem.at[i])

    def start_chunk(i, carry):
        wq_copy(i).start()
        wkv_copy(i).start()
        return carry

    lax.fori_loop(0, CHUNKS, start_chunk, 0)
    key_copy = pltpu.make_async_copy(keys, k_v, load_sem.at[1])
    value_copy = pltpu.make_async_copy(values, v_v, load_sem.at[2])
    wo_copy = pltpu.make_async_copy(wo, wo_v, load_sem.at[3])
    key_copy.start()
    value_copy.start()
    wo_copy.start()

    for copy in small:
        copy.wait()
    low, high = at_lanes(0, RANK), at_lanes(64, RANK)
    dg[core, chip, 0:64, :] = (dot(down_v[0], low) + dot(down_v[1], high)).astype(bf16)
    dg[core, chip, 64:96, :] = (dot(down_v[2, 0:32, :], low) + dot(down_v[2, 32:64, :], high)).astype(bf16)
    ug[chip, 0:32, :] = (dot_tn(qup_v[...], low) + dot(odown_v[...], high)).astype(bf16)
    ug[chip, 32:64, :] = (dot(oup_v[0:32, :], low) + dot(oup_v[32:64, :], high)).astype(bf16)
    last = dot_tn(kvup_v[1], low) + dot_tn(kvup_v[0], high)
    ug[chip, 64:80, :] = jnp.concatenate([last, jnp.zeros_like(last)], axis=0).astype(bf16)

    pl.semaphore_wait(barrier, CHIPS + TP - 1)

    def d_copy(j):
        return pltpu.make_async_remote_copy(
            src_ref=dg.at[core, chip], dst_ref=dg.at[core, chip],
            send_sem=d_send.at[j], recv_sem=d_recv.at[j],
            device_id=(chip_at(j) * 2 + core, t), device_id_type=MESH)

    def u_copy(j):
        return pltpu.make_async_remote_copy(
            src_ref=ug.at[chip], dst_ref=ug.at[chip],
            send_sem=u_send.at[j], recv_sem=u_recv.at[j],
            device_id=(chip_at(j) * 2 + core, t), device_id_type=MESH)

    for j in range(1, CHIPS):
        d_copy(j).start()
    for j in range(1, CHIPS):
        u_copy(j).start()

    hid_copy.wait()

    def squares(i, total):
        cols = pl.ds(pl.multiple_of(i * CHUNK, CHUNK), CHUNK)
        x = hid_v[:, cols].astype(f32)
        x = x * x
        for k in range(CHUNK // 128):
            total = total + x[:, k * 128 : (k + 1) * 128]
        return total

    total = lax.fori_loop(0, CHUNKS, squares, jnp.zeros((SEQS, 128), f32))
    square = jnp.sum(total, axis=-1, keepdims=True) * (1.0 / FEATURES)
    scale = lax.rsqrt(square + epsilon)

    def normalise(i, carry):
        cols = pl.ds(pl.multiple_of(i * CHUNK, CHUNK), CHUNK)
        x = hid_v[:, cols].astype(f32)
        nrm_v[:, cols] = (x * scale * gain[:, cols].astype(f32)).astype(bf16)
        return carry

    lax.fori_loop(0, CHUNKS, normalise, 0)

    qacc[...] = jnp.zeros_like(qacc)
    kacc[...] = jnp.zeros_like(kacc)
    vacc[...] = jnp.zeros_like(vacc)

    def project(i, carry):
        wq_copy(i).wait()
        wkv_copy(i).wait()
        cols = pl.ds(pl.multiple_of(i * CHUNK, CHUNK), CHUNK)
        x = nrm_v[:, cols]
        qacc[...] += dot(x, wq_v[cols, :])
        kacc[...] += dot(x, wkv_v[0, cols, :])
        vacc[...] += dot(x, wkv_v[1, cols, :])
        return carry

    lax.fori_loop(0, CHUNKS, project, 0)

    w2[...] = jnp.zeros_like(w2)
    for j in range(1, CHIPS):
        d_copy(j).wait_recv()
    across = pltpu.make_async_remote_copy(
        src_ref=dg.at[core], dst_ref=dg.at[core],
        send_sem=dd_sem.at[0], recv_sem=dd_sem.at[1],
        device_id=(partner, t), device_id_type=MESH)
    across.start()

    for j in range(1, CHIPS):
        u_copy(j).wait_recv()

    def t_copy(j):
        return pltpu.make_async_remote_copy(
            src_ref=ug.at[tp_at(j)], dst_ref=ut.at[core, t],
            send_sem=t_send.at[j], recv_sem=t_recv.at[j],
            device_id=(rep, tp_at(j)), device_id_type=MESH)

    lane = lax.broadcasted_iota(jnp.int32, (SEQS, 128), 1)
    half = pl.multiple_of((t % 2) * 64, 64)

    across.wait_recv()
    partial = jnp.zeros((SEQS, 256), f32)
    for r in range(2 * CHIPS):
        c, q = r % 2, r // 2
        w2[r, pl.ds(half, 64), 0:128] = dg[c, q, 0:64, :]
        tail = dg[c, q, 64:96, :].astype(f32)
        both = jnp.concatenate([tail, pltpu.roll(tail, 64, axis=1)], axis=0)
        w2[r, pl.ds(half, 64), 128:256] = both.astype(bf16)
    for r in range(2 * CHIPS):
        cols = pl.ds(pl.multiple_of(r * QCOLS + (t // 2) * 128, 128), 128)
        partial = partial + dot(nrm_v[:, cols], w2[r])
    inner_p[t, 0:64, :] = partial[:, 0:128].astype(bf16)
    tail = partial[:, 128:256]
    tail = jnp.where(lane[0:32] < 64, tail[0:32], pltpu.roll(tail[32:64], 64, axis=1))
    inner_p[t, 64:96, :] = tail.astype(bf16)

    def i_copy(j):
        return pltpu.make_async_remote_copy(
            src_ref=inner_p.at[t], dst_ref=inner_p.at[t],
            send_sem=i_send.at[j], recv_sem=i_recv.at[j],
            device_id=(rep, tp_at(j)), device_id_type=MESH)

    for j in range(1, TP):
        i_copy(j).start()
    for j in range(1, TP):
        t_copy(j).start()
    ut[core, t] = ug[t]

    lens = lengths[...].reshape(1, SEQS)
    square_rows = lax.broadcasted_iota(jnp.int32, (SEQS, SEQS), 0)
    square_lanes = lax.broadcasted_iota(jnp.int32, (SEQS, SEQS), 1)
    len_col = jnp.sum(
        jnp.where(square_rows == square_lanes, jnp.broadcast_to(lens, (SEQS, SEQS)), 0).astype(f32),
        axis=-1, keepdims=True)
    len_b = jnp.broadcast_to(len_col, (SEQS, 128))
    for h in range(8):
        len_s[pl.ds(h, SEQS, stride=8), :] = len_b
    index = (lane % 64).astype(f32)
    frequency = jnp.exp(index * (-2.0 / HEAD * math.log(rope_base)))
    angles = len_b * frequency
    cosine = jnp.cos(angles)
    sine = jnp.where(lane < 64, -jnp.sin(angles), jnp.sin(angles))

    def rotate(x):
        return x * cosine + pltpu.roll(x, 64, axis=1) * sine

    for j in range(1, TP):
        t_copy(j).wait_recv()
    up_across = pltpu.make_async_remote_copy(
        src_ref=ut.at[core], dst_ref=ut.at[core],
        send_sem=tt_sem.at[0], recv_sem=tt_sem.at[1],
        device_id=(partner, t), device_id_type=MESH)
    up_across.start()

    for j in range(1, TP):
        i_copy(j).wait_recv()
    inner = inner_p[0].astype(f32)
    for k in range(1, TP):
        inner = inner + inner_p[k].astype(f32)
    first = inner[0:64]
    tail = inner[64:96]
    tail = jnp.concatenate([tail, pltpu.roll(tail, 64, axis=1)], axis=0)
    inner_q = jnp.where(lane < 64, first, 0.0).astype(bf16)
    inner_k = jnp.where(lane < 64, 0.0, first).astype(bf16)
    inner_v = jnp.where(lane < 64, tail, 0.0).astype(bf16)
    up_across.wait_recv()

    up_rows = ut[:, :, 0:32, :].reshape(QCOLS, 128)
    kv_rows = jnp.concatenate(
        [ut[n // TP, n % TP, 64:80, :].astype(f32)[0:8] for n in range(2 * TP)], axis=0).astype(bf16)
    new_key = rotate(kacc[...] + adapter_scale * dot_nt(inner_k, kv_rows)).astype(bf16).astype(f32)
    new_value = (vacc[...] + adapter_scale * dot_nt(inner_v, kv_rows)).astype(bf16).astype(f32)
    query = qacc[...] + adapter_scale * dot_nt(inner_q, up_rows)
    score_scale = 1.0 / math.sqrt(HEAD)
    for h in range(4):
        x = rotate(query[:, h * HEAD : (h + 1) * HEAD])
        main = x.astype(bf16).astype(f32)
        own = jnp.sum(x * new_key, axis=-1, keepdims=True) * score_scale
        own = jnp.broadcast_to(own, (SEQS, 128))
        q_s[pl.ds(h, SEQS, stride=8), :] = main
        q_s[pl.ds(h + 4, SEQS, stride=8), :] = x - main
        own_s[pl.ds(h, SEQS, stride=8), :] = own
        own_s[pl.ds(h + 4, SEQS, stride=8), :] = own

    key_copy.wait()
    value_copy.wait()
    wide = 8 * GROUP
    position = lax.broadcasted_iota(jnp.int32, (wide, 128), 1).astype(f32)

    def attend(g, carry):
        rows = pl.ds(pl.multiple_of(g * wide, wide), wide)
        q_rows = q_s[rows, :].astype(bf16)
        scores = []
        for s in range(GROUP):
            sc = dot_nt(q_rows[s * 8 : (s + 1) * 8], k_v[g * GROUP + s, 0])
            scores.append(sc + pltpu.roll(sc, 4, axis=0))
        scores = jnp.concatenate(scores, axis=0) * score_scale
        own = own_s[rows, :]
        live = position < len_s[rows, :]
        row_max = jnp.maximum(
            jnp.max(jnp.where(live, scores, -1e30), axis=-1, keepdims=True), own)
        weights = jnp.where(live, jnp.exp(scores - row_max), 0.0)
        own_weight = jnp.exp(own - row_max)
        denom = jnp.sum(weights, axis=-1, keepdims=True) + own_weight
        probs = (weights / denom).astype(bf16)
        own_s[rows, :] = (own_weight / denom).astype(bf16).astype(f32)
        parts = [
            dot(probs[s * 8 : (s + 1) * 8], v_v[g * GROUP + s, 0]) for s in range(GROUP)
        ]
        ctx_s[rows, :] = jnp.concatenate(parts, axis=0)
        return carry

    lax.fori_loop(0, SEQS // GROUP, attend, 0)

    for h in range(4):
        x = ctx_s[pl.ds(h, SEQS, stride=8), :] + own_s[pl.ds(h, SEQS, stride=8), :] * new_value
        ctx_b[:, h * HEAD : (h + 1) * HEAD] = x.astype(bf16)
    context = ctx_b[...]

    middle = dot(context, up_rows)
    middle = jnp.where(lane[0:32] < 64, pltpu.roll(middle[0:32], 64, axis=1), middle[32:64])
    mid_p[t] = middle

    def m_copy(j):
        return pltpu.make_async_remote_copy(
            src_ref=mid_p.at[t], dst_ref=mid_p.at[t],
            send_sem=m_send.at[j], recv_sem=m_recv.at[j],
            device_id=(rep, tp_at(j)), device_id_type=MESH)

    for j in range(1, TP):
        m_copy(j).start()
    wo_copy.wait()

    def r_copy(j):
        return pltpu.make_async_remote_copy(
            src_ref=rs_send.at[tp_at(j)], dst_ref=rs_recv.at[t],
            send_sem=r_send.at[j], recv_sem=r_recv.at[j],
            device_id=(rep, tp_at(j)), device_id_type=MESH)

    def send_block(j, carry):
        cols = pl.ds(pl.multiple_of(tp_at(j) * OUTC, OUTC), OUTC)
        rs_send[tp_at(j)] = dot(ctx_b[...], wo_v[:, cols]).astype(bf16)
        r_copy(j).start()
        return carry

    lax.fori_loop(1, TP, send_block, 0)

    for k in range(TP):
        a = ut[(2 * k) // TP, (2 * k) % TP, 32:64, :].astype(f32)
        b = ut[(2 * k) // TP, (2 * k + 1) % TP, 32:64, :].astype(f32)
        a_r, b_r = pltpu.roll(a, 64, axis=1), pltpu.roll(b, 64, axis=1)
        left = lane[0:32] < 64
        ou_v[0:32, k * 128 : (k + 1) * 128] = jnp.where(left, a, b_r).astype(bf16)
        ou_v[32:64, k * 128 : (k + 1) * 128] = jnp.where(left, a_r, b).astype(bf16)

    mine = pl.ds(pl.multiple_of(t * OUTC, OUTC), OUTC)
    own_block = dot(ctx_b[...], wo_v[:, mine])

    for j in range(1, TP):
        m_copy(j).wait_recv()
    middle = mid_p[0]
    for k in range(1, TP):
        middle = middle + mid_p[k]
    middle = jnp.concatenate([middle, pltpu.roll(middle, 64, axis=1)], axis=0)[:, 0:64].astype(bf16)
    out_v[...] = own_block + adapter_scale * dot(middle, ou_v[...])

    def add_block(j, carry):
        r_copy(j).wait_recv()
        out_v[...] += rs_recv[lax.rem(t + TP - j, TP)].astype(f32)
        return carry

    lax.fori_loop(1, TP, add_block, 0)
    out[...] = out_v[...].astype(bf16)

    for j in range(1, CHIPS):
        d_copy(j).wait_send()
        u_copy(j).wait_send()
    across.wait_send()
    up_across.wait_send()
    for j in range(1, TP):
        i_copy(j).wait_send()
        t_copy(j).wait_send()
        m_copy(j).wait_send()
        r_copy(j).wait_send()


def local(
    hidden, norm_gain, query_weight_matrix, key_value_weight, output_weight_matrix,
    input_down_factors, query_up_factor, key_value_up_factors, output_down_factor,
    output_up_factor, cache_keys, cache_values, lengths,
):
    anywhere = pl.BlockSpec(memory_space=pl.ANY)
    vmem = pl.BlockSpec(memory_space=pltpu.VMEM)
    dma = pltpu.SemaphoreType.DMA
    return pl.pallas_call(
        kernel,
        out_shape=jax.ShapeDtypeStruct((SEQS, OUTC), bf16),
        in_specs=[anywhere, vmem] + [anywhere] * 10 + [vmem],
        out_specs=vmem,
        scratch_shapes=[
            pltpu.VMEM((SEQS, FEATURES), bf16),
            pltpu.VMEM((SEQS, FEATURES), bf16),
            pltpu.VMEM((FEATURES, QCOLS), bf16),
            pltpu.VMEM((2, FEATURES, HEAD), bf16),
            pltpu.VMEM((QCOLS, FEATURES), bf16),
            pltpu.VMEM((SEQS, 1, 128, HEAD), bf16),
            pltpu.VMEM((SEQS, 1, 128, HEAD), bf16),
            pltpu.VMEM((3, 64, RANK), bf16),
            pltpu.VMEM((RANK, 32), bf16),
            pltpu.VMEM((2, RANK, 8), bf16),
            pltpu.VMEM((32, RANK), bf16),
            pltpu.VMEM((RANK, 64), bf16),
            pltpu.VMEM((2, CHIPS, DROWS, 128), bf16),
            pltpu.VMEM((2 * CHIPS, 128, 256), bf16),
            pltpu.VMEM((CHIPS, UROWS, 128), bf16),
            pltpu.VMEM((2, TP, UROWS, 128), bf16),
            pltpu.VMEM((TP, DROWS, 128), bf16),
            pltpu.VMEM((RANK, OUTC), bf16),
            pltpu.VMEM((TP, 32, 128), f32),
            pltpu.VMEM((TP, SEQS, OUTC), bf16),
            pltpu.VMEM((TP, SEQS, OUTC), bf16),
            pltpu.VMEM((SEQS, QCOLS), f32),
            pltpu.VMEM((SEQS, HEAD), f32),
            pltpu.VMEM((SEQS, HEAD), f32),
            pltpu.VMEM((SEQS * 8, HEAD), f32),
            pltpu.VMEM((SEQS * 8, HEAD), f32),
            pltpu.VMEM((SEQS * 8, HEAD), f32),
            pltpu.VMEM((SEQS * 8, HEAD), f32),
            pltpu.VMEM((SEQS, QCOLS), bf16),
            pltpu.VMEM((SEQS, OUTC), f32),
            dma((4,)), dma((CHUNKS,)), dma((CHUNKS,)), dma((5,)),
            dma((CHIPS,)), dma((CHIPS,)), dma((2,)), dma((CHIPS,)), dma((CHIPS,)),
            dma((TP,)), dma((TP,)), dma((2,)),
            dma((TP,)), dma((TP,)), dma((TP,)), dma((TP,)), dma((TP,)), dma((TP,)),
        ],
        compiler_params=pltpu.CompilerParams(
            collective_id=0, has_side_effects=True, vmem_limit_bytes=60 * 1024 * 1024),
        cost_estimate=pl.CostEstimate(
            flops=3 * 10**9, bytes_accessed=26 * 2**20, transcendentals=0),
    )(
        hidden, norm_gain.reshape(1, FEATURES), query_weight_matrix, key_value_weight,
        output_weight_matrix, input_down_factors, query_up_factor, key_value_up_factors,
        output_down_factor, output_up_factor, cache_keys, cache_values, lengths,
    )


def solution(mesh):
    placed = (
        P("rep", None),
        P(),
        P(None, "tp"),
        P(None, None, "tp"),
        P("tp", None),
        P(None, ("rep", "tp"), None),
        P(None, ("rep", "tp")),
        P(None, None, ("rep", "tp")),
        P(("rep", "tp"), None),
        P(None, ("rep", "tp")),
        P("rep", "tp", None, None),
        P("rep", "tp", None, None),
        P("rep"),
    )
    return jax.shard_map(
        local, mesh=mesh, in_specs=placed, out_specs=P("rep", "tp"), check_vma=False
    )
```

time: 184 us -> 52.7 us (0.29)
  the two profiles are of different devices: /device:TPU:0 before, /device:TPU:1 now
where the time goes in v1:
time: 52.7 us; the launch traced here: 52.4 us
  Pallas kernels  46.7 us (89%)
  local copies, waits for them, and re-layouts  5.67 us (11%)
    pallas_call x1, Pallas kernels, local(): pl.pallas_call(kernel, out_shape=jax.ShapeDtypeStruct((SEQS, OUTC), bf16)...  46.7 us
    unnamed x3, local copies, waits for them, and re-layouts  4.32 us
    reshape x1, local copies, waits for them, and re-layouts, local(): norm_gain.reshape(1, FEATURES)  1.35 us

profile of v1, /device:TPU:1, one launch (start us, length us, event | category | flops | bytes accessed | tf_op | source)
XLA Modules:
  0.0 52.4 jit_solution(1799844019290949211)
XLA Ops:
  0.0 1.4 %copy.14.qup = bf16[64,32]{1,0:T(8,128)(2,1)} copy(bf16[64,32]{0,1:T(8,128)(2,1)} %param.19) | data formatting | bytes 8192 | tf_op args[6]
  1.4 1.3 %reshape.3.gain = bf16[1,8192]{1,0:T(2,128)(2,1)} reshape(bf16[8192]{0:T(1024)(128)(2,1)} %param.14) | data formatting | bytes 32768 | tf_op jit(solution)/shard_map/reshape | solution.py:440
  2.7 1.4 %copy.15.kvup = bf16[2,64,8]{2,1,0:T(8,128)(2,1)} copy(bf16[2,64,8]{1,2,0:T(8,128)(2,1)} %param.20) | data formatting | bytes 4096 | tf_op args[7]
  4.1 46.7 %shard_map.127 = bf16[64,1024]{1,0:T(8,128)(2,1)} custom-call(bf16[64,8192]{1,0:T(8,128)(2,1)} %hidden.1, bf16[1,8192]{1,0:T(2,128)(2,1)} %reshape.3.gain, bf16[8192,512]{1,0:T(8,128)(2,1)} %wq.1, bf16[2,8192,128]{2,1,0:T(8,128)(2,1)} %wkv.1, bf16[512,8192]{1,0:T(8,128)(2,1)} %wo.1, bf16[3,64,64]{2,1,0:T(8,128)(2,1)} %down.1, bf16[64,32]{1,0:T(8,128)(2,1)} %copy.14.qup, ...), custom_call_target="tpu_custom_call" | custom-call | flops 3000000000 | bytes 27262976 | tf_op jit(solution)/shard_map/pallas_call | solution.py:394
  50.8 1.6 %copy.17 = bf16[64,1024]{1,0:T(8,128)(2,1)} copy(bf16[64,1024]{1,0:T(8,128)(2,1)} %shard_map.127) | data formatting | bytes 262144

commit v2 on v1

v2 whole, which is shorter than its diff:
```python
import math

import jax
import jax.numpy as jnp
from jax import lax
from jax.experimental import pallas as pl
from jax.experimental.pallas import tpu as pltpu
from jax.sharding import PartitionSpec as P

MESH = pl.DeviceIdType.MESH
bf16, f32 = jnp.bfloat16, jnp.float32

epsilon = 1e-06
rope_base = 1000000.0
adapter_scale = 0.5

FEATURES = 8192
SEQS = 64
RANK = 64
HEAD = 128
QCOLS = 512
OUTC = 1024
TP = 8
CHIPS = 8
CHUNKS = 8
CHUNK = FEATURES // CHUNKS
DROWS = 96
UROWS = 80
GROUP = 16
PART = 512


def dot(a, b):
    return jnp.dot(a, b, preferred_element_type=f32)


def dot_nt(a, b):
    return lax.dot_general(a, b, (((1,), (1,)), ((), ())), preferred_element_type=f32)


def at_lanes(offset, rows):
    row = lax.broadcasted_iota(jnp.int32, (rows, 128), 0)
    lane = lax.broadcasted_iota(jnp.int32, (rows, 128), 1)
    return jnp.where(lane == row + offset, 1.0, 0.0).astype(bf16)


def kernel(
    hidden, gain, wq, wkv, wo, down, qup, kvup, odown, oup, keys, values, lengths,
    out,
    hid_v, nrm_v, wq_v, wkv_v, wo_v, k_v, v_v,
    down_v, qup_v, kvup_v, odown_v, oup_v, gain_v, len_v,
    dg, w2, ug, ute, utl, inner_p, inner_v, ou_v, od_v, mid_p,
    xs0, xr0, z1s, z1r, o1s, o1r, y1s, y1r, xs1, xr1, z0s, z0r, o0s, o0r, y0s, y0r,
    own1, own0, qacc, kacc, vacc, q_s, own_s, ctx_s, len_s, ctx_b,
    load_sem, wq_sem, wkv_sem, small_sem,
    d_send, d_recv, dd_sem, u_send, u_recv, t_send, t_recv, tt_sem, l_send, l_recv, ll_sem,
    i_send, i_recv, v_send, v_recv, m_send, m_recv,
    x0_send, x0_recv, x1_sem, z_send, z_recv,
):
    rep = lax.axis_index("rep")
    t = lax.axis_index("tp")
    chip = rep // 2
    core = rep % 2
    partner = chip * 2 + (1 - core)
    a, k = t // 4, t % 4
    other = 1 - a

    def chip_at(j):
        return lax.rem(chip + j, CHIPS)

    def tp_at(j):
        return lax.rem(t + j, TP)

    def z_at(d):
        return lax.rem(k + d, 4)

    def remote(src, dst, send_sem, recv_sem, rep_to, tp_to):
        return pltpu.make_async_remote_copy(
            src_ref=src, dst_ref=dst, send_sem=send_sem, recv_sem=recv_sem,
            device_id=(rep_to, tp_to), device_id_type=MESH)

    barrier = pltpu.get_barrier_semaphore()
    small = [
        pltpu.make_async_copy(src, dst, small_sem.at[i])
        for i, (src, dst) in enumerate(
            ((down, down_v), (qup, qup_v), (kvup, kvup_v), (odown, odown_v), (oup, oup_v),
             (gain, gain_v), (lengths, len_v))
        )
    ]
    small[0].start()
    pl.semaphore_signal(barrier, inc=1, device_id=(partner, t), device_id_type=MESH)
    for j in range(1, CHIPS):
        pl.semaphore_signal(barrier, inc=1, device_id=(chip_at(j) * 2 + core, t), device_id_type=MESH)
    for j in range(1, TP):
        pl.semaphore_signal(barrier, inc=1, device_id=(rep, tp_at(j)), device_id_type=MESH)
    for copy in small[1:]:
        copy.start()
    hid_copy = pltpu.make_async_copy(hidden, hid_v, load_sem.at[0])
    hid_copy.start()

    def wq_copy(i):
        rows = pl.ds(pl.multiple_of(i * CHUNK, CHUNK), CHUNK)
        return pltpu.make_async_copy(wq.at[rows, :], wq_v.at[rows, :], wq_sem.at[i])

    def wkv_copy(i):
        rows = pl.ds(pl.multiple_of(i * CHUNK, CHUNK), CHUNK)
        return pltpu.make_async_copy(wkv.at[:, rows, :], wkv_v.at[:, rows, :], wkv_sem.at[i])

    def start_chunk(i, carry):
        wq_copy(i).start()
        wkv_copy(i).start()
        return carry

    lax.fori_loop(0, CHUNKS, start_chunk, 0)
    key_copy = pltpu.make_async_copy(keys, k_v, load_sem.at[1])
    value_copy = pltpu.make_async_copy(values, v_v, load_sem.at[2])
    wo_copy = pltpu.make_async_copy(wo, wo_v, load_sem.at[3])
    key_copy.start()
    value_copy.start()
    wo_copy.start()

    low, high = at_lanes(0, RANK), at_lanes(64, RANK)
    with jax.named_scope("pack"):
        small[0].wait()
        dg[core, chip, 0:64, :] = (dot(down_v[0], low) + dot(down_v[1], high)).astype(bf16)
        dg[core, chip, 64:96, :] = (dot(down_v[2, 0:32, :], low) + dot(down_v[2, 32:64, :], high)).astype(bf16)
        for copy in small[1:]:
            copy.wait()
        ug[chip, 0:16, :] = (dot(qup_v[0:16, :], low) + dot(qup_v[16:32, :], high)).astype(bf16)
        last = dot(kvup_v[1], low) + dot(kvup_v[0], high)
        ug[chip, 16:32, :] = jnp.concatenate([last, jnp.zeros_like(last)], axis=0).astype(bf16)
        ug[chip, 32:48, :] = (dot(odown_v[0:16, :], low) + dot(odown_v[16:32, :], high)).astype(bf16)
        ug[chip, 48:80, :] = (dot(oup_v[0:32, :], low) + dot(oup_v[32:64, :], high)).astype(bf16)

    with jax.named_scope("barrier_wait"):
        pl.semaphore_wait(barrier, CHIPS + TP - 1)

    def d_copy(j):
        return remote(dg.at[core, chip], dg.at[core, chip], d_send.at[j], d_recv.at[j],
                      chip_at(j) * 2 + core, t)

    def u_copy(j):
        return remote(ug.at[chip], ug.at[chip], u_send.at[j], u_recv.at[j],
                      chip_at(j) * 2 + core, t)

    for j in range(1, CHIPS):
        d_copy(j).start()
    for j in range(1, CHIPS):
        u_copy(j).start()

    with jax.named_scope("hid_wait"):
        hid_copy.wait()

    def squares(i, total):
        cols = pl.ds(pl.multiple_of(i * CHUNK, CHUNK), CHUNK)
        x = hid_v[:, cols].astype(f32)
        x = x * x
        for n in range(CHUNK // 128):
            total = total + x[:, n * 128 : (n + 1) * 128]
        return total

    with jax.named_scope("norm"):
        total = lax.fori_loop(0, CHUNKS, squares, jnp.zeros((SEQS, 128), f32))
        square = jnp.sum(total, axis=-1, keepdims=True) * (1.0 / FEATURES)
        scale = lax.rsqrt(square + epsilon)

        def normalise(i, carry):
            cols = pl.ds(pl.multiple_of(i * CHUNK, CHUNK), CHUNK)
            x = hid_v[:, cols].astype(f32)
            nrm_v[:, cols] = (x * scale * gain_v[cols].astype(f32).reshape(1, CHUNK)).astype(bf16)
            return carry

        lax.fori_loop(0, CHUNKS, normalise, 0)

    w2[...] = jnp.zeros_like(w2)
    qacc[...] = jnp.zeros_like(qacc)
    kacc[...] = jnp.zeros_like(kacc)
    vacc[...] = jnp.zeros_like(vacc)

    def project(i, carry):
        wq_copy(i).wait()
        wkv_copy(i).wait()
        cols = pl.ds(pl.multiple_of(i * CHUNK, CHUNK), CHUNK)
        x = nrm_v[:, cols]
        qacc[...] += dot(x, wq_v[cols, :])
        kacc[...] += dot(x, wkv_v[0, cols, :])
        vacc[...] += dot(x, wkv_v[1, cols, :])
        return carry

    with jax.named_scope("project"):
        lax.fori_loop(0, CHUNKS, project, 0)

    lane = lax.broadcasted_iota(jnp.int32, (SEQS, 128), 1)
    left = lane < 64
    with jax.named_scope("angles"):
        lens = len_v[...].reshape(1, SEQS)
        square_rows = lax.broadcasted_iota(jnp.int32, (SEQS, SEQS), 0)
        square_lanes = lax.broadcasted_iota(jnp.int32, (SEQS, SEQS), 1)
        len_col = jnp.sum(
            jnp.where(square_rows == square_lanes, jnp.broadcast_to(lens, (SEQS, SEQS)), 0).astype(f32),
            axis=-1, keepdims=True)
        len_b = jnp.broadcast_to(len_col, (SEQS, 128))
        for h in range(8):
            len_s[pl.ds(h, SEQS, stride=8), :] = len_b
        index = (lane % 64).astype(f32)
        frequency = jnp.exp(index * (-2.0 / HEAD * math.log(rope_base)))
        angles = len_b * frequency
        cosine = jnp.cos(angles)
        sine = jnp.where(left, -jnp.sin(angles), jnp.sin(angles))

    def rotate(x):
        return x * cosine + pltpu.roll(x, 64, axis=1) * sine

    with jax.named_scope("d_wait"):
        for j in range(1, CHIPS):
            d_copy(j).wait_recv()
    across = remote(dg.at[core], dg.at[core], dd_sem.at[0], dd_sem.at[1], partner, t)
    across.start()

    half = pl.multiple_of((t % 2) * 64, 64)

    def spread(c):
        for q in range(CHIPS):
            w2[c, q, pl.ds(half, 64), 0:128] = dg[c, q, 0:64, :]
            tail = dg[c, q, 64:96, :].astype(f32)
            both = jnp.concatenate([tail, pltpu.roll(tail, 64, axis=1)], axis=0)
            w2[c, q, pl.ds(half, 64), 128:256] = both.astype(bf16)

    def features(c):
        total = jnp.zeros((SEQS, 256), f32)
        for q in range(CHIPS):
            at = (q * 2 + c) * QCOLS + (t // 2) * 128
            total = total + dot(nrm_v[:, pl.ds(pl.multiple_of(at, 128), 128)], w2[c, q])
        return total

    with jax.named_scope("inner_own"):
        spread(core)
        partial = features(core)

    with jax.named_scope("u_wait"):
        for j in range(1, CHIPS):
            u_copy(j).wait_recv()

    def t_copy(j):
        return remote(ug.at[tp_at(j), 0:32], ute.at[core, t], t_send.at[j], t_recv.at[j], rep, tp_at(j))

    def l_copy(j):
        return remote(ug.at[tp_at(j), 32:80], utl.at[core, t], l_send.at[j], l_recv.at[j], rep, tp_at(j))

    for j in range(1, TP):
        t_copy(j).start()
    ute[core, t] = ug[t, 0:32]
    utl[core, t] = ug[t, 32:80]

    with jax.named_scope("across_wait"):
        across.wait_recv()
    with jax.named_scope("inner_other"):
        spread(1 - core)
        partial = partial + features(1 - core)
        inner_p[t] = partial[:, 0:128].astype(bf16)
        tail = partial[:, 128:256]
        tail = jnp.where(left[0:32], tail[0:32], pltpu.roll(tail[32:64], 64, axis=1))
        inner_v[t] = tail.astype(bf16)

    def i_copy(j):
        return remote(inner_p.at[t], inner_p.at[t], i_send.at[j], i_recv.at[j], rep, tp_at(j))

    def v_copy(j):
        return remote(inner_v.at[t], inner_v.at[t], v_send.at[j], v_recv.at[j], rep, tp_at(j))

    for j in range(1, TP):
        i_copy(j).start()
    for j in range(1, TP):
        v_copy(j).start()
    for j in range(1, TP):
        l_copy(j).start()

    with jax.named_scope("t_wait"):
        for j in range(1, TP):
            t_copy(j).wait_recv()
    t_across = remote(ute.at[core], ute.at[core], tt_sem.at[0], tt_sem.at[1], partner, t)
    t_across.start()
    with jax.named_scope("up_wait"):
        t_across.wait_recv()
    with jax.named_scope("unpack"):
        rows = []
        for n in range(2 * TP):
            e = ute[n // TP, n % TP, 0:16, :].astype(f32)
            rows += [e, pltpu.roll(e, 64, axis=1)]
        up_rows = jnp.concatenate(rows, axis=0).astype(bf16)
        kv_rows = jnp.concatenate(
            [ute[n // TP, n % TP, 16:32, :].astype(f32)[0:8] for n in range(2 * TP)], axis=0).astype(bf16)

    with jax.named_scope("i_wait"):
        for j in range(1, TP):
            i_copy(j).wait_recv()
    score_scale = 1.0 / math.sqrt(HEAD)
    with jax.named_scope("queries"):
        inner = inner_p[0].astype(f32)
        for n in range(1, TP):
            inner = inner + inner_p[n].astype(f32)
        inner_q = jnp.where(left, inner, 0.0).astype(bf16)
        inner_k = jnp.where(left, 0.0, inner).astype(bf16)
        new_key = rotate(kacc[...] + adapter_scale * dot_nt(inner_k, kv_rows)).astype(bf16).astype(f32)
        query = qacc[...] + adapter_scale * dot_nt(inner_q, up_rows)
        for h in range(4):
            x = rotate(query[:, h * HEAD : (h + 1) * HEAD])
            main = x.astype(bf16).astype(f32)
            own = jnp.sum(x * new_key, axis=-1, keepdims=True) * score_scale
            own = jnp.broadcast_to(own, (SEQS, 128))
            q_s[pl.ds(h, SEQS, stride=8), :] = main
            q_s[pl.ds(h + 4, SEQS, stride=8), :] = x - main
            own_s[pl.ds(h, SEQS, stride=8), :] = own
            own_s[pl.ds(h + 4, SEQS, stride=8), :] = own

    with jax.named_scope("late_wait"):
        for j in range(1, TP):
            v_copy(j).wait_recv()
        for j in range(1, TP):
            l_copy(j).wait_recv()
    l_across = remote(utl.at[core], utl.at[core], ll_sem.at[0], ll_sem.at[1], partner, t)
    l_across.start()

    with jax.named_scope("cache_wait"):
        key_copy.wait()
        value_copy.wait()
    wide = 8 * GROUP
    position = lax.broadcasted_iota(jnp.int32, (wide, 128), 1).astype(f32)

    def attend(g, carry):
        rows = pl.ds(pl.multiple_of(g * wide, wide), wide)
        q_rows = q_s[rows, :].astype(bf16)
        scores = []
        for s in range(GROUP):
            sc = dot_nt(q_rows[s * 8 : (s + 1) * 8], k_v[g * GROUP + s, 0])
            scores.append(sc + pltpu.roll(sc, 4, axis=0))
        scores = jnp.concatenate(scores, axis=0) * score_scale
        own = own_s[rows, :]
        live = position < len_s[rows, :]
        row_max = jnp.maximum(
            jnp.max(jnp.where(live, scores, -1e30), axis=-1, keepdims=True), own)
        weights = jnp.where(live, jnp.exp(scores - row_max), 0.0)
        own_weight = jnp.exp(own - row_max)
        denom = jnp.sum(weights, axis=-1, keepdims=True) + own_weight
        probs = (weights / denom).astype(bf16)
        own_s[rows, :] = (own_weight / denom).astype(bf16).astype(f32)
        parts = [
            dot(probs[s * 8 : (s + 1) * 8], v_v[g * GROUP + s, 0]) for s in range(GROUP)
        ]
        ctx_s[rows, :] = jnp.concatenate(parts, axis=0)
        return carry

    with jax.named_scope("attend"):
        lax.fori_loop(0, SEQS // GROUP, attend, 0)

    with jax.named_scope("context"):
        l_across.wait_recv()
        inner = inner_v[0].astype(f32)
        for n in range(1, TP):
            inner = inner + inner_v[n].astype(f32)
        inner = jnp.concatenate([inner, pltpu.roll(inner, 64, axis=1)], axis=0)
        inner = jnp.where(left, inner, 0.0).astype(bf16)
        new_value = (vacc[...] + adapter_scale * dot_nt(inner, kv_rows)).astype(bf16).astype(f32)
        for h in range(4):
            x = ctx_s[pl.ds(h, SEQS, stride=8), :] + own_s[pl.ds(h, SEQS, stride=8), :] * new_value
            ctx_b[:, h * HEAD : (h + 1) * HEAD] = x.astype(bf16)

    def m_copy(j):
        return remote(mid_p.at[t], mid_p.at[t], m_send.at[j], m_recv.at[j], rep, tp_at(j))

    with jax.named_scope("middle"):
        for n in range(2 * TP):
            e = utl[n // TP, n % TP, 0:16, :].astype(f32)
            e = jnp.concatenate([e, pltpu.roll(e, 64, axis=1)], axis=0)
            od_v[n * 32 : (n + 1) * 32, :] = e.astype(bf16)
        middle = dot(ctx_b[...], od_v[...])
        middle = jnp.where(left[0:32], middle[0:32], pltpu.roll(middle[32:64], 64, axis=1))
        mid_p[t] = middle.astype(bf16)
        for j in range(1, TP):
            m_copy(j).start()

    with jax.named_scope("wo_wait"):
        wo_copy.wait()

    z_minus, z_plus = a * 4 + z_at(3), a * 4 + z_at(1)
    across_x = other * 4 + k

    def block(a_to, d, part):
        at = (a_to * 4 + z_at(d)) * OUTC + part * PART
        return dot(ctx_b[...], wo_v[:, pl.ds(pl.multiple_of(at, PART), PART)])

    def x0_copy(d):
        return remote(xs0.at[d], xr0.at[d], x0_send.at[d], x0_recv.at[d], rep, across_x)

    x1_copy = remote(xs1, xr1, x1_sem.at[0], x1_sem.at[1], rep, across_x)

    def z_copy(src, dst, n, way):
        return remote(src.at[way], dst.at[way], z_send.at[n, way], z_recv.at[n, way],
                      rep, z_minus if way == 0 else z_plus)

    with jax.named_scope("send1"):
        for a_to in range(2):
            x = block(a_to, 2, 1).astype(bf16)
            z1s[0, :, a_to * PART : (a_to + 1) * PART] = x[0:32]
            z1s[1, :, a_to * PART : (a_to + 1) * PART] = x[32:64]
        for way in range(2):
            z_copy(z1s, z1r, 0, way).start()
    with jax.named_scope("send2"):
        for d in (2, 3, 1, 0):
            xs0[d] = block(other, d, 0).astype(bf16)
            x0_copy(d).start()
    with jax.named_scope("send3"):
        for way, d in ((0, 3), (1, 1)):
            for a_to in range(2):
                cols = slice(a_to * PART, (a_to + 1) * PART)
                x = block(a_to, d, 1)
                sent, kept = (x[32:64], x[0:32]) if way == 0 else (x[0:32], x[32:64])
                o1s[way, :, cols] = sent.astype(bf16)
                own1[way, :, cols] = kept
            z_copy(o1s, o1r, 1, way).start()
    with jax.named_scope("own"):
        for d in (2, 3, 1, 0):
            own0[d] = block(a, d, 0)
    with jax.named_scope("relay1"):
        for way in range(2):
            z_copy(z1s, z1r, 0, way).wait_recv()
            y1s[way] = (own1[way] + z1r[way].astype(f32)).astype(bf16)
            z_copy(y1s, y1r, 2, way).start()
    with jax.named_scope("xfirst"):
        x0_copy(2).wait_recv()
        x = (own0[2] + xr0[2].astype(f32)).astype(bf16)
        z0s[0], z0s[1] = x[0:32], x[32:64]
        for way in range(2):
            z_copy(z0s, z0r, 3, way).start()
        for way, d in ((0, 3), (1, 1)):
            x0_copy(d).wait_recv()
            x = own0[d] + xr0[d].astype(f32)
            sent, kept = (x[32:64], x[0:32]) if way == 0 else (x[0:32], x[32:64])
            o0s[way] = sent.astype(bf16)
            own0[d, 0:32] = kept
            z_copy(o0s, o0r, 4, way).start()
    with jax.named_scope("relay0"):
        for way, d in ((0, 3), (1, 1)):
            z_copy(z0s, z0r, 3, way).wait_recv()
            y0s[way] = (own0[d, 0:32] + z0r[way].astype(f32)).astype(bf16)
            z_copy(y0s, y0r, 5, way).start()
    with jax.named_scope("own1"):
        mine = [block(other, 0, 1), block(a, 0, 1)]
    with jax.named_scope("ou"):
        for n in range(TP):
            e = utl[(2 * n) // TP, (2 * n) % TP, 16:48, :].astype(f32)
            g = utl[(2 * n) // TP, (2 * n + 1) % TP, 16:48, :].astype(f32)
            e_r, g_r = pltpu.roll(e, 64, axis=1), pltpu.roll(g, 64, axis=1)
            ou_v[0:32, n * 128 : (n + 1) * 128] = jnp.where(left[0:32], e, g_r).astype(bf16)
            ou_v[32:64, n * 128 : (n + 1) * 128] = jnp.where(left[0:32], e_r, g).astype(bf16)
    with jax.named_scope("m_wait"):
        for j in range(1, TP):
            m_copy(j).wait_recv()
    with jax.named_scope("delta"):
        middle = mid_p[0].astype(f32)
        for n in range(1, TP):
            middle = middle + mid_p[n].astype(f32)
        middle = jnp.concatenate([middle, pltpu.roll(middle, 64, axis=1)], axis=0)[:, 0:64].astype(bf16)
        delta = adapter_scale * dot(middle, ou_v[...])
    with jax.named_scope("z1_wait"):
        for way in range(2):
            z_copy(o1s, o1r, 1, way).wait_recv()
        for way in range(2):
            z_copy(y1s, y1r, 2, way).wait_recv()
    with jax.named_scope("sum1"):

        def arrived(a_to):
            cols = pl.ds(pl.multiple_of(a_to * PART, PART), PART)
            top = y1r[0, :, cols].astype(f32) + o1r[1, :, cols].astype(f32)
            bottom = y1r[1, :, cols].astype(f32) + o1r[0, :, cols].astype(f32)
            return jnp.concatenate([top, bottom], axis=0)

        xs1[...] = (mine[0] + arrived(other)).astype(bf16)
        x1_copy.start()
        high_half = mine[1] + arrived(a) + delta[:, PART:]
    with jax.named_scope("z0_wait"):
        x0_copy(0).wait_recv()
        for way in range(2):
            z_copy(o0s, o0r, 4, way).wait_recv()
        for way in range(2):
            z_copy(y0s, y0r, 5, way).wait_recv()
    with jax.named_scope("sum0"):
        top = y0r[0].astype(f32) + o0r[1].astype(f32)
        bottom = y0r[1].astype(f32) + o0r[0].astype(f32)
        x = own0[0] + xr0[0].astype(f32) + jnp.concatenate([top, bottom], axis=0)
        out[:, 0:PART] = (x + delta[:, 0:PART]).astype(bf16)
    with jax.named_scope("x1_wait"):
        x1_copy.wait_recv()
    out[:, PART:] = (high_half + xr1[...].astype(f32)).astype(bf16)

    with jax.named_scope("drain"):
        for j in range(1, CHIPS):
            d_copy(j).wait_send()
            u_copy(j).wait_send()
        across.wait_send()
        t_across.wait_send()
        l_across.wait_send()
        for j in range(1, TP):
            i_copy(j).wait_send()
            v_copy(j).wait_send()
            t_copy(j).wait_send()
            l_copy(j).wait_send()
            m_copy(j).wait_send()
        for d in range(4):
            x0_copy(d).wait_send()
        x1_copy.wait_send()
        for way in range(2):
            for n, (src, dst) in enumerate(
                ((z1s, z1r), (o1s, o1r), (y1s, y1r), (z0s, z0r), (o0s, o0r), (y0s, y0r))
            ):
                z_copy(src, dst, n, way).wait_send()


def local(
    hidden, norm_gain, query_weight_matrix, key_value_weight, output_weight_matrix,
    input_down_factors, query_up_factor, key_value_up_factors, output_down_factor,
    output_up_factor, cache_keys, cache_values, lengths,
):
    hbm = pl.BlockSpec(memory_space=pltpu.HBM)
    dma = pltpu.SemaphoreType.DMA
    vmem = pltpu.VMEM
    half_block = vmem((2, 32, OUTC), bf16)
    half_part = vmem((2, 32, PART), bf16)
    return pl.pallas_call(
        kernel,
        out_shape=jax.ShapeDtypeStruct((SEQS, OUTC), bf16),
        in_specs=[hbm] * 13,
        out_specs=pl.BlockSpec(memory_space=pltpu.VMEM),
        scratch_shapes=[
            vmem((SEQS, FEATURES), bf16),
            vmem((SEQS, FEATURES), bf16),
            vmem((FEATURES, QCOLS), bf16),
            vmem((2, FEATURES, HEAD), bf16),
            vmem((QCOLS, FEATURES), bf16),
            vmem((SEQS, 1, 128, HEAD), bf16),
            vmem((SEQS, 1, 128, HEAD), bf16),
            vmem((3, 64, RANK), bf16),
            vmem((32, RANK), bf16),
            vmem((2, 8, RANK), bf16),
            vmem((32, RANK), bf16),
            vmem((RANK, 64), bf16),
            vmem((FEATURES,), bf16),
            vmem((SEQS,), jnp.int32),
            vmem((2, CHIPS, DROWS, 128), bf16),
            vmem((2, CHIPS, 128, 256), bf16),
            vmem((CHIPS, UROWS, 128), bf16),
            vmem((2, TP, 32, 128), bf16),
            vmem((2, TP, 48, 128), bf16),
            vmem((TP, SEQS, 128), bf16),
            vmem((TP, 32, 128), bf16),
            vmem((RANK, OUTC), bf16),
            vmem((QCOLS, 128), bf16),
            vmem((TP, 32, 128), bf16),
            vmem((4, SEQS, PART), bf16),
            vmem((4, SEQS, PART), bf16),
            half_block, half_block, half_block, half_block, half_block, half_block,
            vmem((SEQS, PART), bf16),
            vmem((SEQS, PART), bf16),
            half_part, half_part, half_part, half_part, half_part, half_part,
            vmem((2, 32, OUTC), f32),
            vmem((4, SEQS, PART), f32),
            vmem((SEQS, QCOLS), f32),
            vmem((SEQS, HEAD), f32),
            vmem((SEQS, HEAD), f32),
            vmem((SEQS * 8, HEAD), f32),
            vmem((SEQS * 8, HEAD), f32),
            vmem((SEQS * 8, HEAD), f32),
            vmem((SEQS * 8, HEAD), f32),
            vmem((SEQS, QCOLS), bf16),
            dma((4,)), dma((CHUNKS,)), dma((CHUNKS,)), dma((7,)),
            dma((CHIPS,)), dma((CHIPS,)), dma((2,)), dma((CHIPS,)), dma((CHIPS,)),
            dma((TP,)), dma((TP,)), dma((2,)), dma((TP,)), dma((TP,)), dma((2,)),
            dma((TP,)), dma((TP,)), dma((TP,)), dma((TP,)), dma((TP,)), dma((TP,)),
            dma((4,)), dma((4,)), dma((2,)), dma((6, 2)), dma((6, 2)),
        ],
        compiler_params=pltpu.CompilerParams(
            collective_id=0, has_side_effects=True, vmem_limit_bytes=48 * 1024 * 1024),
        cost_estimate=pl.CostEstimate(
            flops=3 * 10**9, bytes_accessed=26 * 2**20, transcendentals=0),
    )(*[pltpu.with_memory_space_constraint(x, pltpu.HBM) for x in (
        hidden, norm_gain, query_weight_matrix, key_value_weight,
        output_weight_matrix, input_down_factors, jnp.swapaxes(query_up_factor, 0, 1),
        jnp.swapaxes(key_value_up_factors, 1, 2), output_down_factor, output_up_factor,
        cache_keys, cache_values, lengths,
    )])


def solution(mesh):
    placed = (
        P("rep", None),
        P(),
        P(None, "tp"),
        P(None, None, "tp"),
        P("tp", None),
        P(None, ("rep", "tp"), None),
        P(None, ("rep", "tp")),
        P(None, None, ("rep", "tp")),
        P(("rep", "tp"), None),
        P(None, ("rep", "tp")),
        P("rep", "tp", None, None),
        P("rep", "tp", None, None),
        P("rep"),
    )
    return jax.shard_map(
        local, mesh=mesh, in_specs=placed, out_specs=P("rep", "tp"), check_vma=False
    )
```

time: 52.7 us -> 39.8 us (0.76)
  the two profiles are of different devices: /device:TPU:1 before, /device:TPU:0 now
where the time goes in v2:
time: 39.8 us; the launch traced here: 39.7 us
  Pallas kernels  39 us (98%)
  local copies, waits for them, and re-layouts  0.66 us (2%)
    pallas_call x1, Pallas kernels, local(): pl.pallas_call(kernel, out_shape=jax.ShapeDtypeStruct((SEQS, OUTC), bf16)...  39 us

profile of v2, /device:TPU:0, one launch (start us, length us, event | category | flops | bytes accessed | tf_op | source)
XLA Modules:
  0.0 39.7 jit_solution(2156343695025104475)
XLA Ops:
  0.0 39.0 %shard_map.127 = bf16[64,1024]{1,0:T(8,128)(2,1)S(1)} custom-call(bf16[64,8192]{1,0:T(8,128)(2,1)} %hidden.1, bf16[8192]{0:T(1024)(128)(2,1)} %gain.1, bf16[8192,512]{1,0:T(8,128)(2,1)} %wq.1, bf16[2,8192,128]{2,1,0:T(8,128)(2,1)} %wkv.1, bf16[512,8192]{1,0:T(8,128)(2,1)} %wo.1, bf16[3,64,64]{2,1,0:T(8,128)(2,1)} %down.1, bf16[32,64]{1,0:T(8,128)(2,1)} %bitcast.2, ...), custom_call_target="tpu_custom_call" | custom-call | flops 3000000000 | bytes 27262976 | tf_op jit(solution)/shard_map/pallas_call | solution.py:529
  39.1 0.7 %copy.15 = bf16[64,1024]{1,0:T(8,128)(2,1)} copy(bf16[64,1024]{1,0:T(8,128)(2,1)S(1)} %shard_map.127) | data formatting | bytes 262144

commit v3 on v2

--- a/solution.py
+++ b/solution.py
@@ -26,7 +26,7 @@
 CHUNK = FEATURES // CHUNKS
 DROWS = 96
 UROWS = 80
-GROUP = 16
+GROUP = 32
 PART = 512
 
 
@@ -50,10 +50,9 @@
     hid_v, nrm_v, wq_v, wkv_v, wo_v, k_v, v_v,
     down_v, qup_v, kvup_v, odown_v, oup_v, gain_v, len_v,
     dg, w2, ug, ute, utl, inner_p, inner_v, ou_v, od_v, mid_p,
-    xs0, xr0, z1s, z1r, o1s, o1r, y1s, y1r, xs1, xr1, z0s, z0r, o0s, o0r, y0s, y0r,
-    own1, own0, qacc, kacc, vacc, q_s, own_s, ctx_s, len_s, ctx_b,
+    xs0, xr0, zs, zr, xs1, xr1, kept, own0, mine, qacc, kacc, vacc, q_s, own_s, ctx_s, len_s, ctx_b,
     load_sem, wq_sem, wkv_sem, small_sem,
-    d_send, d_recv, dd_sem, u_send, u_recv, t_send, t_recv, tt_sem, l_send, l_recv, ll_sem,
+    d_send, d_recv, dd_send, dd_recv, u_send, u_recv, t_send, t_recv, tt_sem, l_send, l_recv, ll_sem,
     i_send, i_recv, v_send, v_recv, m_send, m_recv,
     x0_send, x0_recv, x1_sem, z_send, z_recv,
 ):
@@ -67,6 +66,14 @@
 
     def chip_at(j):
         return lax.rem(chip + j, CHIPS)
+
+    def tp_of(j):
+        return t if j % 2 == 0 else lax.rem(t + 4, TP)
+
+    def gather_peer(j):
+        return chip_at(j) * 2 + core, tp_of(j)
+
+    far_first = (4, 3, 5, 1, 7, 2, 6)
 
     def tp_at(j):
         return lax.rem(t + j, TP)
@@ -90,7 +97,7 @@
     small[0].start()
     pl.semaphore_signal(barrier, inc=1, device_id=(partner, t), device_id_type=MESH)
     for j in range(1, CHIPS):
-        pl.semaphore_signal(barrier, inc=1, device_id=(chip_at(j) * 2 + core, t), device_id_type=MESH)
+        pl.semaphore_signal(barrier, inc=1, device_id=gather_peer(j), device_id_type=MESH)
     for j in range(1, TP):
         pl.semaphore_signal(barrier, inc=1, device_id=(rep, tp_at(j)), device_id_type=MESH)
     for copy in small[1:]:
@@ -137,15 +144,20 @@
 
     def d_copy(j):
         return remote(dg.at[core, chip], dg.at[core, chip], d_send.at[j], d_recv.at[j],
-                      chip_at(j) * 2 + core, t)
+                      *gather_peer(j))
 
     def u_copy(j):
         return remote(ug.at[chip], ug.at[chip], u_send.at[j], u_recv.at[j],
-                      chip_at(j) * 2 + core, t)
-
-    for j in range(1, CHIPS):
+                      *gather_peer(j))
+
+    def across(j):
+        q = lax.rem(chip + CHIPS - j, CHIPS)
+        return remote(dg.at[core, q], dg.at[core, q], dd_send.at[j], dd_recv.at[j], partner, t)
+
+    for j in far_first:
         d_copy(j).start()
-    for j in range(1, CHIPS):
+    across(0).start()
+    for j in far_first:
         u_copy(j).start()
 
     with jax.named_scope("hid_wait"):
@@ -214,8 +226,7 @@
     with jax.named_scope("d_wait"):
         for j in range(1, CHIPS):
             d_copy(j).wait_recv()
-    across = remote(dg.at[core], dg.at[core], dd_sem.at[0], dd_sem.at[1], partner, t)
-    across.start()
+            across(j).start()
 
     half = pl.multiple_of((t % 2) * 64, 64)
 
@@ -228,9 +239,9 @@
 
     def features(c):
         total = jnp.zeros((SEQS, 256), f32)
-        for q in range(CHIPS):
-            at = (q * 2 + c) * QCOLS + (t // 2) * 128
-            total = total + dot(nrm_v[:, pl.ds(pl.multiple_of(at, 128), 128)], w2[c, q])
+        for j in range(CHIPS):
+            at = (chip_at(j) * 2 + c) * QCOLS + (tp_of(j) // 2) * 128
+            total = total + dot(nrm_v[:, pl.ds(pl.multiple_of(at, 128), 128)], w2[c, chip_at(j)])
         return total
 
     with jax.named_scope("inner_own"):
@@ -241,19 +252,25 @@
         for j in range(1, CHIPS):
             u_copy(j).wait_recv()
 
+    def slot_for(to):
+        return lax.rem(t + 4 * lax.rem(to + chip, 2), TP)
+
     def t_copy(j):
-        return remote(ug.at[tp_at(j), 0:32], ute.at[core, t], t_send.at[j], t_recv.at[j], rep, tp_at(j))
+        to = tp_at(j)
+        return remote(ug.at[to, 0:32], ute.at[core, slot_for(to)], t_send.at[j], t_recv.at[j], rep, to)
 
     def l_copy(j):
-        return remote(ug.at[tp_at(j), 32:80], utl.at[core, t], l_send.at[j], l_recv.at[j], rep, tp_at(j))
+        to = tp_at(j)
+        return remote(ug.at[to, 32:80], utl.at[core, slot_for(to)], l_send.at[j], l_recv.at[j], rep, to)
 
     for j in range(1, TP):
         t_copy(j).start()
-    ute[core, t] = ug[t, 0:32]
-    utl[core, t] = ug[t, 32:80]
+    ute[core, slot_for(t)] = ug[t, 0:32]
+    utl[core, slot_for(t)] = ug[t, 32:80]
 
     with jax.named_scope("across_wait"):
-        across.wait_recv()
+        for j in range(CHIPS):
+            across(j).wait_recv()
     with jax.named_scope("inner_other"):
         spread(1 - core)
         partial = partial + features(1 - core)
@@ -312,14 +329,6 @@
             q_s[pl.ds(h + 4, SEQS, stride=8), :] = x - main
             own_s[pl.ds(h, SEQS, stride=8), :] = own
             own_s[pl.ds(h + 4, SEQS, stride=8), :] = own
-
-    with jax.named_scope("late_wait"):
-        for j in range(1, TP):
-            v_copy(j).wait_recv()
-        for j in range(1, TP):
-            l_copy(j).wait_recv()
-    l_across = remote(utl.at[core], utl.at[core], ll_sem.at[0], ll_sem.at[1], partner, t)
-    l_across.start()
 
     with jax.named_scope("cache_wait"):
         key_copy.wait()
@@ -351,10 +360,23 @@
         return carry
 
     with jax.named_scope("attend"):
-        lax.fori_loop(0, SEQS // GROUP, attend, 0)
+        lax.fori_loop(0, SEQS // GROUP // 2, attend, 0)
+    with jax.named_scope("late_wait"):
+        for j in range(1, TP):
+            v_copy(j).wait_recv()
+        for j in range(1, TP):
+            l_copy(j).wait_recv()
+    l_across = remote(utl.at[core], utl.at[core], ll_sem.at[0], ll_sem.at[1], partner, t)
+    l_across.start()
+    with jax.named_scope("attend2"):
+        lax.fori_loop(SEQS // GROUP // 2, SEQS // GROUP, attend, 0)
 
     with jax.named_scope("context"):
         l_across.wait_recv()
+        for n in range(2 * TP):
+            e = utl[n // TP, n % TP, 0:16, :].astype(f32)
+            e = jnp.concatenate([e, pltpu.roll(e, 64, axis=1)], axis=0)
+            od_v[n * 32 : (n + 1) * 32, :] = e.astype(bf16)
         inner = inner_v[0].astype(f32)
         for n in range(1, TP):
             inner = inner + inner_v[n].astype(f32)
@@ -365,87 +387,108 @@
             x = ctx_s[pl.ds(h, SEQS, stride=8), :] + own_s[pl.ds(h, SEQS, stride=8), :] * new_value
             ctx_b[:, h * HEAD : (h + 1) * HEAD] = x.astype(bf16)
 
-    def m_copy(j):
-        return remote(mid_p.at[t], mid_p.at[t], m_send.at[j], m_recv.at[j], rep, tp_at(j))
-
-    with jax.named_scope("middle"):
-        for n in range(2 * TP):
-            e = utl[n // TP, n % TP, 0:16, :].astype(f32)
-            e = jnp.concatenate([e, pltpu.roll(e, 64, axis=1)], axis=0)
-            od_v[n * 32 : (n + 1) * 32, :] = e.astype(bf16)
-        middle = dot(ctx_b[...], od_v[...])
-        middle = jnp.where(left[0:32], middle[0:32], pltpu.roll(middle[32:64], 64, axis=1))
-        mid_p[t] = middle.astype(bf16)
-        for j in range(1, TP):
-            m_copy(j).start()
-
     with jax.named_scope("wo_wait"):
         wo_copy.wait()
 
     z_minus, z_plus = a * 4 + z_at(3), a * 4 + z_at(1)
     across_x = other * 4 + k
+    top, bottom = slice(0, 32), slice(32, 64)
 
     def block(a_to, d, part):
         at = (a_to * 4 + z_at(d)) * OUTC + part * PART
         return dot(ctx_b[...], wo_v[:, pl.ds(pl.multiple_of(at, PART), PART)])
 
+    def field(f, d):
+        return block(other, d, 1) if f == 1 else block(a, d, 1 if f == 2 else 0)
+
     def x0_copy(d):
         return remote(xs0.at[d], xr0.at[d], x0_send.at[d], x0_recv.at[d], rep, across_x)
 
     x1_copy = remote(xs1, xr1, x1_sem.at[0], x1_sem.at[1], rep, across_x)
 
-    def z_copy(src, dst, n, way):
-        return remote(src.at[way], dst.at[way], z_send.at[n, way], z_recv.at[n, way],
-                      rep, z_minus if way == 0 else z_plus)
-
+    def z_copy(f, kind, way):
+        return remote(zs.at[f, kind, way], zr.at[f, kind, way], z_send.at[f, kind, way],
+                      z_recv.at[f, kind, way], rep, z_minus if way == 0 else z_plus)
+
+    def far(f, x):
+        zs[f, 0, 0] = x[top].astype(bf16)
+        zs[f, 0, 1] = x[bottom].astype(bf16)
+        for way in range(2):
+            z_copy(f, 0, way).start()
+
+    def near(f, way, x):
+        zs[f, 1, way] = (x[bottom] if way == 0 else x[top]).astype(bf16)
+        kept[f, way] = x[top] if way == 0 else x[bottom]
+        z_copy(f, 1, way).start()
+
+    def relay(f, way):
+        z_copy(f, 0, way).wait_recv()
+        zs[f, 2, way] = (kept[f, way] + zr[f, 0, way].astype(f32)).astype(bf16)
+        z_copy(f, 2, way).start()
+
+    def arrived(f):
+        for kind in (1, 2):
+            for way in range(2):
+                z_copy(f, kind, way).wait_recv()
+        first = zr[f, 2, 0].astype(f32) + zr[f, 1, 1].astype(f32)
+        last = zr[f, 2, 1].astype(f32) + zr[f, 1, 0].astype(f32)
+        return jnp.concatenate([first, last], axis=0)
+
+    def x_first(d):
+        xs0[d] = block(other, d, 0).astype(bf16)
+        x0_copy(d).start()
+
+    def m_copy(src, dst, n, to):
+        return remote(mid_p.at[src], mid_p.at[dst], m_send.at[n], m_recv.at[n], rep, to)
+
+    m_x = m_copy(0, 1, 0, across_x)
+    m_minus = m_copy(2, 3, 1, z_minus)
+    m_plus = m_copy(2, 4, 2, z_plus)
+    m_two = m_copy(2, 5, 3, a * 4 + z_at(2))
+
+    with jax.named_scope("send0"):
+        far(1, field(1, 2))
+    with jax.named_scope("middle"):
+        middle = dot(ctx_b[...], od_v[...])
+        middle = jnp.where(left[0:32], middle[0:32], pltpu.roll(middle[32:64], 64, axis=1))
+        mid_p[0] = middle.astype(bf16)
+        m_x.start()
     with jax.named_scope("send1"):
-        for a_to in range(2):
-            x = block(a_to, 2, 1).astype(bf16)
-            z1s[0, :, a_to * PART : (a_to + 1) * PART] = x[0:32]
-            z1s[1, :, a_to * PART : (a_to + 1) * PART] = x[32:64]
-        for way in range(2):
-            z_copy(z1s, z1r, 0, way).start()
+        x_first(2)
+        far(2, field(2, 2))
+        x_first(3)
+        near(1, 0, field(1, 3))
+        near(1, 1, field(1, 1))
+        x_first(1)
+        near(2, 0, field(2, 3))
+        near(2, 1, field(2, 1))
     with jax.named_scope("send2"):
-        for d in (2, 3, 1, 0):
-            xs0[d] = block(other, d, 0).astype(bf16)
-            x0_copy(d).start()
-    with jax.named_scope("send3"):
-        for way, d in ((0, 3), (1, 1)):
-            for a_to in range(2):
-                cols = slice(a_to * PART, (a_to + 1) * PART)
-                x = block(a_to, d, 1)
-                sent, kept = (x[32:64], x[0:32]) if way == 0 else (x[0:32], x[32:64])
-                o1s[way, :, cols] = sent.astype(bf16)
-                own1[way, :, cols] = kept
-            z_copy(o1s, o1r, 1, way).start()
-    with jax.named_scope("own"):
-        for d in (2, 3, 1, 0):
-            own0[d] = block(a, d, 0)
+        x_first(0)
+        own0[0] = field(0, 2)
+        own0[1] = field(0, 3)
+        own0[2] = field(0, 1)
     with jax.named_scope("relay1"):
         for way in range(2):
-            z_copy(z1s, z1r, 0, way).wait_recv()
-            y1s[way] = (own1[way] + z1r[way].astype(f32)).astype(bf16)
-            z_copy(y1s, y1r, 2, way).start()
-    with jax.named_scope("xfirst"):
+            relay(1, way)
+    with jax.named_scope("own"):
+        mine[1] = field(1, 0)
+        mine[0] = field(0, 0)
+        mine[2] = field(2, 0)
+    with jax.named_scope("mid_x"):
+        m_x.wait_recv()
+        mid_p[2] = (mid_p[0].astype(f32) + mid_p[1].astype(f32)).astype(bf16)
+        m_two.start()
+        m_minus.start()
+        m_plus.start()
+    with jax.named_scope("x_far"):
         x0_copy(2).wait_recv()
-        x = (own0[2] + xr0[2].astype(f32)).astype(bf16)
-        z0s[0], z0s[1] = x[0:32], x[32:64]
+        far(0, own0[0] + xr0[2].astype(f32))
+    with jax.named_scope("relay2"):
         for way in range(2):
-            z_copy(z0s, z0r, 3, way).start()
-        for way, d in ((0, 3), (1, 1)):
-            x0_copy(d).wait_recv()
-            x = own0[d] + xr0[d].astype(f32)
-            sent, kept = (x[32:64], x[0:32]) if way == 0 else (x[0:32], x[32:64])
-            o0s[way] = sent.astype(bf16)
-            own0[d, 0:32] = kept
-            z_copy(o0s, o0r, 4, way).start()
-    with jax.named_scope("relay0"):
-        for way, d in ((0, 3), (1, 1)):
-            z_copy(z0s, z0r, 3, way).wait_recv()
-            y0s[way] = (own0[d, 0:32] + z0r[way].astype(f32)).astype(bf16)
-            z_copy(y0s, y0r, 5, way).start()
-    with jax.named_scope("own1"):
-        mine = [block(other, 0, 1), block(a, 0, 1)]
+            relay(2, way)
+    with jax.named_scope("x_near0"):
+        x0_copy(3).wait_recv()
+        near(0, 0, own0[1] + xr0[3].astype(f32))
     with jax.named_scope("ou"):
         for n in range(TP):
             e = utl[(2 * n) // TP, (2 * n) % TP, 16:48, :].astype(f32)
@@ -453,51 +496,39 @@
             e_r, g_r = pltpu.roll(e, 64, axis=1), pltpu.roll(g, 64, axis=1)
             ou_v[0:32, n * 128 : (n + 1) * 128] = jnp.where(left[0:32], e, g_r).astype(bf16)
             ou_v[32:64, n * 128 : (n + 1) * 128] = jnp.where(left[0:32], e_r, g).astype(bf16)
-    with jax.named_scope("m_wait"):
-        for j in range(1, TP):
-            m_copy(j).wait_recv()
+    with jax.named_scope("done1"):
+        xs1[...] = (mine[1] + arrived(1)).astype(bf16)
+        x1_copy.start()
+    with jax.named_scope("x_near1"):
+        x0_copy(1).wait_recv()
+        near(0, 1, own0[2] + xr0[1].astype(f32))
+    with jax.named_scope("relay0"):
+        for way in range(2):
+            relay(0, way)
+    with jax.named_scope("done2"):
+        mine[2] = mine[2] + arrived(2)
     with jax.named_scope("delta"):
-        middle = mid_p[0].astype(f32)
-        for n in range(1, TP):
+        for copy in (m_minus, m_plus, m_two):
+            copy.wait_recv()
+        middle = mid_p[2].astype(f32)
+        for n in range(3, 6):
             middle = middle + mid_p[n].astype(f32)
         middle = jnp.concatenate([middle, pltpu.roll(middle, 64, axis=1)], axis=0)[:, 0:64].astype(bf16)
         delta = adapter_scale * dot(middle, ou_v[...])
-    with jax.named_scope("z1_wait"):
-        for way in range(2):
-            z_copy(o1s, o1r, 1, way).wait_recv()
-        for way in range(2):
-            z_copy(y1s, y1r, 2, way).wait_recv()
-    with jax.named_scope("sum1"):
-
-        def arrived(a_to):
-            cols = pl.ds(pl.multiple_of(a_to * PART, PART), PART)
-            top = y1r[0, :, cols].astype(f32) + o1r[1, :, cols].astype(f32)
-            bottom = y1r[1, :, cols].astype(f32) + o1r[0, :, cols].astype(f32)
-            return jnp.concatenate([top, bottom], axis=0)
-
-        xs1[...] = (mine[0] + arrived(other)).astype(bf16)
-        x1_copy.start()
-        high_half = mine[1] + arrived(a) + delta[:, PART:]
-    with jax.named_scope("z0_wait"):
+    with jax.named_scope("done0"):
         x0_copy(0).wait_recv()
-        for way in range(2):
-            z_copy(o0s, o0r, 4, way).wait_recv()
-        for way in range(2):
-            z_copy(y0s, y0r, 5, way).wait_recv()
-    with jax.named_scope("sum0"):
-        top = y0r[0].astype(f32) + o0r[1].astype(f32)
-        bottom = y0r[1].astype(f32) + o0r[0].astype(f32)
-        x = own0[0] + xr0[0].astype(f32) + jnp.concatenate([top, bottom], axis=0)
-        out[:, 0:PART] = (x + delta[:, 0:PART]).astype(bf16)
+        x = mine[0] + xr0[0].astype(f32) + delta[:, 0:PART]
+        out[:, 0:PART] = (x + arrived(0)).astype(bf16)
     with jax.named_scope("x1_wait"):
         x1_copy.wait_recv()
-    out[:, PART:] = (high_half + xr1[...].astype(f32)).astype(bf16)
+    out[:, PART:] = (mine[2] + delta[:, PART:] + xr1[...].astype(f32)).astype(bf16)
 
     with jax.named_scope("drain"):
         for j in range(1, CHIPS):
             d_copy(j).wait_send()
             u_copy(j).wait_send()
-        across.wait_send()
+        for j in range(CHIPS):
+            across(j).wait_send()
         t_across.wait_send()
         l_across.wait_send()
         for j in range(1, TP):
@@ -505,15 +536,15 @@
             v_copy(j).wait_send()
             t_copy(j).wait_send()
             l_copy(j).wait_send()
-            m_copy(j).wait_send()
+        for copy in (m_x, m_minus, m_plus, m_two):
+            copy.wait_send()
         for d in range(4):
             x0_copy(d).wait_send()
         x1_copy.wait_send()
-        for way in range(2):
-            for n, (src, dst) in enumerate(
-                ((z1s, z1r), (o1s, o1r), (y1s, y1r), (z0s, z0r), (o0s, o0r), (y0s, y0r))
-            ):
-                z_copy(src, dst, n, way).wait_send()
+        for f in range(3):
+            for kind in range(3):
+                for way in range(2):
+                    z_copy(f, kind, way).wait_send()
 
 
 def local(
@@ -524,8 +555,6 @@
     hbm = pl.BlockSpec(memory_space=pltpu.HBM)
     dma = pltpu.SemaphoreType.DMA
     vmem = pltpu.VMEM
-    half_block = vmem((2, 32, OUTC), bf16)
-    half_part = vmem((2, 32, PART), bf16)
     return pl.pallas_call(
         kernel,
         out_shape=jax.ShapeDtypeStruct((SEQS, OUTC), bf16),
@@ -555,15 +584,16 @@
             vmem((TP, 32, 128), bf16),
             vmem((RANK, OUTC), bf16),
             vmem((QCOLS, 128), bf16),
-            vmem((TP, 32, 128), bf16),
+            vmem((6, 32, 128), bf16),
             vmem((4, SEQS, PART), bf16),
             vmem((4, SEQS, PART), bf16),
-            half_block, half_block, half_block, half_block, half_block, half_block,
+            vmem((3, 3, 2, 32, PART), bf16),
+            vmem((3, 3, 2, 32, PART), bf16),
             vmem((SEQS, PART), bf16),
             vmem((SEQS, PART), bf16),
-            half_part, half_part, half_part, half_part, half_part, half_part,
-            vmem((2, 32, OUTC), f32),
-            vmem((4, SEQS, PART), f32),
+            vmem((3, 2, 32, PART), f32),
+            vmem((3, SEQS, PART), f32),
+            vmem((3, SEQS, PART), f32),
             vmem((SEQS, QCOLS), f32),
             vmem((SEQS, HEAD), f32),
             vmem((SEQS, HEAD), f32),
@@ -573,10 +603,10 @@
             vmem((SEQS * 8, HEAD), f32),
             vmem((SEQS, QCOLS), bf16),
             dma((4,)), dma((CHUNKS,)), dma((CHUNKS,)), dma((7,)),
-            dma((CHIPS,)), dma((CHIPS,)), dma((2,)), dma((CHIPS,)), dma((CHIPS,)),
+            dma((CHIPS,)), dma((CHIPS,)), dma((CHIPS,)), dma((CHIPS,)), dma((CHIPS,)), dma((CHIPS,)),
             dma((TP,)), dma((TP,)), dma((2,)), dma((TP,)), dma((TP,)), dma((2,)),
-            dma((TP,)), dma((TP,)), dma((TP,)), dma((TP,)), dma((TP,)), dma((TP,)),
-            dma((4,)), dma((4,)), dma((2,)), dma((6, 2)), dma((6, 2)),
+            dma((TP,)), dma((TP,)), dma((TP,)), dma((TP,)), dma((4,)), dma((4,)),
+            dma((4,)), dma((4,)), dma((2,)), dma((3, 3, 2)), dma((3, 3, 2)),
         ],
         compiler_params=pltpu.CompilerParams(
             collective_id=0, has_side_effects=True, vmem_limit_bytes=48 * 1024 * 1024),

time: 39.8 us -> 36.2 us (0.910)
  Pallas kernels: 39 us -> 35.5 us
    pallas_call x1, Pallas kernels: 39 us -> 35.5 us  [local(): pl.pallas_call(kernel, out_shape=jax.ShapeDtypeStruct((SEQS, OUTC), bf16)...]
where the time goes in v3:
time: 36.2 us; the launch traced here: 36.1 us
  Pallas kernels  35.5 us (98%)
  local copies, waits for them, and re-layouts  0.66 us (2%)
    pallas_call x1, Pallas kernels, local(): pl.pallas_call(kernel, out_shape=jax.ShapeDtypeStruct((SEQS, OUTC), bf16)...  35.5 us

profile of v3, /device:TPU:0, one launch (start us, length us, event | category | flops | bytes accessed | tf_op | source)
XLA Modules:
  0.0 36.1 jit_solution(2857615438880800936)
XLA Ops:
  0.0 35.5 %shard_map.127 = bf16[64,1024]{1,0:T(8,128)(2,1)S(1)} custom-call(bf16[64,8192]{1,0:T(8,128)(2,1)} %hidden.1, bf16[8192]{0:T(1024)(128)(2,1)} %gain.1, bf16[8192,512]{1,0:T(8,128)(2,1)} %wq.1, bf16[2,8192,128]{2,1,0:T(8,128)(2,1)} %wkv.1, bf16[512,8192]{1,0:T(8,128)(2,1)} %wo.1, bf16[3,64,64]{2,1,0:T(8,128)(2,1)} %down.1, bf16[32,64]{1,0:T(8,128)(2,1)} %bitcast.2, ...), custom_call_target="tpu_custom_call" | custom-call | flops 3000000000 | bytes 27262976 | tf_op jit(solution)/shard_map/pallas_call | solution.py:558
  35.5 0.7 %copy.15 = bf16[64,1024]{1,0:T(8,128)(2,1)} copy(bf16[64,1024]{1,0:T(8,128)(2,1)S(1)} %shard_map.127) | data formatting | bytes 262144

commit v4 on v3

--- a/solution.py
+++ b/solution.py
@@ -28,6 +28,7 @@
 UROWS = 80
 GROUP = 32
 PART = 512
+SLIM = 256
 
 
 def dot(a, b):
@@ -49,13 +50,19 @@
     out,
     hid_v, nrm_v, wq_v, wkv_v, wo_v, k_v, v_v,
     down_v, qup_v, kvup_v, odown_v, oup_v, gain_v, len_v,
-    dg, w2, ug, ute, utl, inner_p, inner_v, ou_v, od_v, mid_p,
-    xs0, xr0, zs, zr, xs1, xr1, kept, own0, mine, qacc, kacc, vacc, q_s, own_s, ctx_s, len_s, ctx_b,
-    load_sem, wq_sem, wkv_sem, small_sem,
-    d_send, d_recv, dd_send, dd_recv, u_send, u_recv, t_send, t_recv, tt_sem, l_send, l_recv, ll_sem,
-    i_send, i_recv, v_send, v_recv, m_send, m_recv,
-    x0_send, x0_recv, x1_sem, z_send, z_recv,
+    dg, w2, ug, ute, utl, uto, inner_p, inner_v, ou_v, od_v, mid_p,
+    xs0, xr0, zs, zr, hs, hr, xs1, xr1, kept, kept_h, own0, mine, qacc, kacc, vacc, q_s, max_s, sum_s, ctx_s, len_s, ctx_b,
+    load_sem, wq_sem, small_sem,
+    d_recv, x0_recv, x1_recv, far_recv, near_recv, sems,
 ):
+    names = ("d_send across_send across_recv u_send u_recv e_send e_recv w_send w_recv t_send t_recv "
+             "tt_send tt_recv l_send l_recv ll_send ll_recv o_send o_recv oo_send oo_recv i_send i_recv "
+             "v_send v_recv m_send m_x m_z x0_send x1_send slim_send wide_send").split()
+    sem = {name: sems.at[n] for n, name in enumerate(names)}
+
+    def wait(ref, name):
+        pltpu.make_async_copy(ref, ref, sem[name]).wait()
+
     rep = lax.axis_index("rep")
     t = lax.axis_index("tp")
     chip = rep // 2
@@ -111,7 +118,7 @@
 
     def wkv_copy(i):
         rows = pl.ds(pl.multiple_of(i * CHUNK, CHUNK), CHUNK)
-        return pltpu.make_async_copy(wkv.at[:, rows, :], wkv_v.at[:, rows, :], wkv_sem.at[i])
+        return pltpu.make_async_copy(wkv.at[:, rows, :], wkv_v.at[:, rows, :], wq_sem.at[i])
 
     def start_chunk(i, carry):
         wq_copy(i).start()
@@ -143,22 +150,32 @@
         pl.semaphore_wait(barrier, CHIPS + TP - 1)
 
     def d_copy(j):
-        return remote(dg.at[core, chip], dg.at[core, chip], d_send.at[j], d_recv.at[j],
+        return remote(dg.at[core, chip], dg.at[core, chip], sem["d_send"], d_recv.at[j],
                       *gather_peer(j))
 
     def u_copy(j):
-        return remote(ug.at[chip], ug.at[chip], u_send.at[j], u_recv.at[j],
-                      *gather_peer(j))
+        piece = ug.at[chip, 0:32]
+        return remote(piece, piece, sem["u_send"], sem["u_recv"], *gather_peer(j))
+
+    def e_copy(j):
+        piece = ug.at[chip, 32:48]
+        return remote(piece, piece, sem["e_send"], sem["e_recv"], *gather_peer(j))
+
+    def w_copy(j):
+        piece = ug.at[chip, 48:80]
+        return remote(piece, piece, sem["w_send"], sem["w_recv"], *gather_peer(j))
 
     def across(j):
         q = lax.rem(chip + CHIPS - j, CHIPS)
-        return remote(dg.at[core, q], dg.at[core, q], dd_send.at[j], dd_recv.at[j], partner, t)
-
+        return remote(dg.at[core, q], dg.at[core, q], sem["across_send"], sem["across_recv"], partner, t)
+
+    for j in far_first:
+        u_copy(j).start()
     for j in far_first:
         d_copy(j).start()
     across(0).start()
     for j in far_first:
-        u_copy(j).start()
+        e_copy(j).start()
 
     with jax.named_scope("hid_wait"):
         hid_copy.wait()
@@ -190,8 +207,8 @@
     vacc[...] = jnp.zeros_like(vacc)
 
     def project(i, carry):
-        wq_copy(i).wait()
-        wkv_copy(i).wait()
+        chunk = wq_v.at[0 : CHUNK * 3 // 2]
+        pltpu.make_async_copy(chunk, chunk, wq_sem.at[i]).wait()
         cols = pl.ds(pl.multiple_of(i * CHUNK, CHUNK), CHUNK)
         x = nrm_v[:, cols]
         qacc[...] += dot(x, wq_v[cols, :])
@@ -223,10 +240,31 @@
     def rotate(x):
         return x * cosine + pltpu.roll(x, 64, axis=1) * sine
 
+    def slot_for(to):
+        return lax.rem(t + 4 * lax.rem(to + chip, 2), TP)
+
+    def t_copy(j):
+        to = tp_at(j)
+        return remote(ug.at[to, 0:32], ute.at[core, slot_for(to)], sem["t_send"], sem["t_recv"], rep, to)
+
+    def l_copy(j):
+        to = tp_at(j)
+        return remote(ug.at[to, 32:48], utl.at[core, slot_for(to)], sem["l_send"], sem["l_recv"], rep, to)
+
+    def o_copy(j):
+        to = tp_at(j)
+        return remote(ug.at[to, 48:80], uto.at[core, slot_for(to)], sem["o_send"], sem["o_recv"], rep, to)
+
+    with jax.named_scope("u_wait"):
+        wait(ug.at[0:7, 0:32], "u_recv")
+        for j in range(1, TP):
+            t_copy(j).start()
     with jax.named_scope("d_wait"):
         for j in range(1, CHIPS):
             d_copy(j).wait_recv()
             across(j).start()
+    for j in far_first:
+        w_copy(j).start()
 
     half = pl.multiple_of((t % 2) * 64, 64)
 
@@ -248,57 +286,39 @@
         spread(core)
         partial = features(core)
 
-    with jax.named_scope("u_wait"):
-        for j in range(1, CHIPS):
-            u_copy(j).wait_recv()
-
-    def slot_for(to):
-        return lax.rem(t + 4 * lax.rem(to + chip, 2), TP)
-
-    def t_copy(j):
-        to = tp_at(j)
-        return remote(ug.at[to, 0:32], ute.at[core, slot_for(to)], t_send.at[j], t_recv.at[j], rep, to)
-
-    def l_copy(j):
-        to = tp_at(j)
-        return remote(ug.at[to, 32:80], utl.at[core, slot_for(to)], l_send.at[j], l_recv.at[j], rep, to)
-
-    for j in range(1, TP):
-        t_copy(j).start()
-    ute[core, slot_for(t)] = ug[t, 0:32]
-    utl[core, slot_for(t)] = ug[t, 32:80]
-
     with jax.named_scope("across_wait"):
-        for j in range(CHIPS):
-            across(j).wait_recv()
+        wait(dg.at[1 - core], "across_recv")
     with jax.named_scope("inner_other"):
         spread(1 - core)
         partial = partial + features(1 - core)
-        inner_p[t] = partial[:, 0:128].astype(bf16)
-        tail = partial[:, 128:256]
-        tail = jnp.where(left[0:32], tail[0:32], pltpu.roll(tail[32:64], 64, axis=1))
-        inner_v[t] = tail.astype(bf16)
+        first, tail = partial[:, 0:128], partial[:, 128:256]
+        packed = jnp.where(left[0:32], first[0:32], pltpu.roll(first[32:64], 64, axis=1))
+        inner_p[t] = packed.astype(bf16)
+        inner_v[t] = jnp.where(left, tail, first).astype(bf16)
 
     def i_copy(j):
-        return remote(inner_p.at[t], inner_p.at[t], i_send.at[j], i_recv.at[j], rep, tp_at(j))
+        return remote(inner_p.at[t], inner_p.at[t], sem["i_send"], sem["i_recv"], rep, tp_at(j))
 
     def v_copy(j):
-        return remote(inner_v.at[t], inner_v.at[t], v_send.at[j], v_recv.at[j], rep, tp_at(j))
+        return remote(inner_v.at[t], inner_v.at[t], sem["v_send"], sem["v_recv"], rep, tp_at(j))
 
     for j in range(1, TP):
         i_copy(j).start()
     for j in range(1, TP):
         v_copy(j).start()
+    with jax.named_scope("w_wait"):
+        wait(ug.at[0:7, 32:48], "e_recv")
     for j in range(1, TP):
         l_copy(j).start()
+    ute[core, slot_for(t)] = ug[t, 0:32]
+    utl[core, slot_for(t)] = ug[t, 32:48]
 
     with jax.named_scope("t_wait"):
-        for j in range(1, TP):
-            t_copy(j).wait_recv()
-    t_across = remote(ute.at[core], ute.at[core], tt_sem.at[0], tt_sem.at[1], partner, t)
+        wait(ute.at[core, 0:7], "t_recv")
+    t_across = remote(ute.at[core], ute.at[core], sem["tt_send"], sem["tt_recv"], partner, t)
     t_across.start()
     with jax.named_scope("up_wait"):
-        t_across.wait_recv()
+        wait(ute.at[1 - core], "tt_recv")
     with jax.named_scope("unpack"):
         rows = []
         for n in range(2 * TP):
@@ -309,26 +329,21 @@
             [ute[n // TP, n % TP, 16:32, :].astype(f32)[0:8] for n in range(2 * TP)], axis=0).astype(bf16)
 
     with jax.named_scope("i_wait"):
-        for j in range(1, TP):
-            i_copy(j).wait_recv()
+        wait(inner_p.at[0:7], "i_recv")
     score_scale = 1.0 / math.sqrt(HEAD)
     with jax.named_scope("queries"):
         inner = inner_p[0].astype(f32)
         for n in range(1, TP):
             inner = inner + inner_p[n].astype(f32)
+        inner = jnp.concatenate([inner, pltpu.roll(inner, 64, axis=1)], axis=0)
         inner_q = jnp.where(left, inner, 0.0).astype(bf16)
-        inner_k = jnp.where(left, 0.0, inner).astype(bf16)
-        new_key = rotate(kacc[...] + adapter_scale * dot_nt(inner_k, kv_rows)).astype(bf16).astype(f32)
         query = qacc[...] + adapter_scale * dot_nt(inner_q, up_rows)
         for h in range(4):
             x = rotate(query[:, h * HEAD : (h + 1) * HEAD])
             main = x.astype(bf16).astype(f32)
-            own = jnp.sum(x * new_key, axis=-1, keepdims=True) * score_scale
-            own = jnp.broadcast_to(own, (SEQS, 128))
             q_s[pl.ds(h, SEQS, stride=8), :] = main
             q_s[pl.ds(h + 4, SEQS, stride=8), :] = x - main
-            own_s[pl.ds(h, SEQS, stride=8), :] = own
-            own_s[pl.ds(h + 4, SEQS, stride=8), :] = own
+            qacc[:, h * HEAD : (h + 1) * HEAD] = x
 
     with jax.named_scope("cache_wait"):
         key_copy.wait()
@@ -344,15 +359,13 @@
             sc = dot_nt(q_rows[s * 8 : (s + 1) * 8], k_v[g * GROUP + s, 0])
             scores.append(sc + pltpu.roll(sc, 4, axis=0))
         scores = jnp.concatenate(scores, axis=0) * score_scale
-        own = own_s[rows, :]
         live = position < len_s[rows, :]
-        row_max = jnp.maximum(
-            jnp.max(jnp.where(live, scores, -1e30), axis=-1, keepdims=True), own)
+        row_max = jnp.max(jnp.where(live, scores, -1e30), axis=-1, keepdims=True)
         weights = jnp.where(live, jnp.exp(scores - row_max), 0.0)
-        own_weight = jnp.exp(own - row_max)
-        denom = jnp.sum(weights, axis=-1, keepdims=True) + own_weight
+        denom = jnp.sum(weights, axis=-1, keepdims=True)
         probs = (weights / denom).astype(bf16)
-        own_s[rows, :] = (own_weight / denom).astype(bf16).astype(f32)
+        max_s[rows, :] = jnp.broadcast_to(row_max, (wide, 128))
+        sum_s[rows, :] = jnp.broadcast_to(denom, (wide, 128))
         parts = [
             dot(probs[s * 8 : (s + 1) * 8], v_v[g * GROUP + s, 0]) for s in range(GROUP)
         ]
@@ -362,33 +375,43 @@
     with jax.named_scope("attend"):
         lax.fori_loop(0, SEQS // GROUP // 2, attend, 0)
     with jax.named_scope("late_wait"):
+        wait(inner_v.at[0:7], "v_recv")
+        wait(utl.at[core, 0:7], "l_recv")
+    l_across = remote(utl.at[core], utl.at[core], sem["ll_send"], sem["ll_recv"], partner, t)
+    l_across.start()
+    with jax.named_scope("o_start"):
+        wait(ug.at[0:7, 48:80], "w_recv")
         for j in range(1, TP):
-            v_copy(j).wait_recv()
-        for j in range(1, TP):
-            l_copy(j).wait_recv()
-    l_across = remote(utl.at[core], utl.at[core], ll_sem.at[0], ll_sem.at[1], partner, t)
-    l_across.start()
+            o_copy(j).start()
     with jax.named_scope("attend2"):
         lax.fori_loop(SEQS // GROUP // 2, SEQS // GROUP, attend, 0)
 
     with jax.named_scope("context"):
-        l_across.wait_recv()
+        wait(utl.at[1 - core], "ll_recv")
         for n in range(2 * TP):
-            e = utl[n // TP, n % TP, 0:16, :].astype(f32)
+            e = utl[n // TP, n % TP].astype(f32)
             e = jnp.concatenate([e, pltpu.roll(e, 64, axis=1)], axis=0)
             od_v[n * 32 : (n + 1) * 32, :] = e.astype(bf16)
         inner = inner_v[0].astype(f32)
         for n in range(1, TP):
             inner = inner + inner_v[n].astype(f32)
-        inner = jnp.concatenate([inner, pltpu.roll(inner, 64, axis=1)], axis=0)
-        inner = jnp.where(left, inner, 0.0).astype(bf16)
-        new_value = (vacc[...] + adapter_scale * dot_nt(inner, kv_rows)).astype(bf16).astype(f32)
+        inner_k = jnp.where(left, 0.0, inner).astype(bf16)
+        new_key = rotate(kacc[...] + adapter_scale * dot_nt(inner_k, kv_rows)).astype(bf16).astype(f32)
+        inner_k = jnp.where(left, inner, 0.0).astype(bf16)
+        new_value = (vacc[...] + adapter_scale * dot_nt(inner_k, kv_rows)).astype(bf16).astype(f32)
         for h in range(4):
-            x = ctx_s[pl.ds(h, SEQS, stride=8), :] + own_s[pl.ds(h, SEQS, stride=8), :] * new_value
+            at = pl.ds(h, SEQS, stride=8)
+            own = jnp.sum(qacc[:, h * HEAD : (h + 1) * HEAD] * new_key, axis=-1, keepdims=True)
+            own = jnp.broadcast_to(own * score_scale, (SEQS, 128))
+            row_max = jnp.maximum(max_s[at, :], own)
+            cached = sum_s[at, :] * jnp.exp(max_s[at, :] - row_max)
+            own = jnp.exp(own - row_max)
+            x = (ctx_s[at, :] * cached + own * new_value) / (cached + own)
             ctx_b[:, h * HEAD : (h + 1) * HEAD] = x.astype(bf16)
 
     with jax.named_scope("wo_wait"):
         wo_copy.wait()
+    o_across = remote(uto.at[core], uto.at[core], sem["oo_send"], sem["oo_recv"], partner, t)
 
     z_minus, z_plus = a * 4 + z_at(3), a * 4 + z_at(1)
     across_x = other * 4 + k
@@ -398,48 +421,57 @@
         at = (a_to * 4 + z_at(d)) * OUTC + part * PART
         return dot(ctx_b[...], wo_v[:, pl.ds(pl.multiple_of(at, PART), PART)])
 
-    def field(f, d):
-        return block(other, d, 1) if f == 1 else block(a, d, 1 if f == 2 else 0)
-
-    def x0_copy(d):
-        return remote(xs0.at[d], xr0.at[d], x0_send.at[d], x0_recv.at[d], rep, across_x)
-
-    x1_copy = remote(xs1, xr1, x1_sem.at[0], x1_sem.at[1], rep, across_x)
+    def x0_copy(n, d):
+        return remote(xs0.at[n, d], xr0.at[n, d], sem["x0_send"], x0_recv.at[n, d], rep, across_x)
+
+    def x1_copy(n):
+        return remote(xs1.at[n], xr1.at[n], sem["x1_send"], x1_recv.at[n], rep, across_x)
+
+    fields = [(hs.at[f], hr.at[f], kept_h.at[f]) for f in range(4)] + [(zs, zr, kept)]
 
     def z_copy(f, kind, way):
-        return remote(zs.at[f, kind, way], zr.at[f, kind, way], z_send.at[f, kind, way],
-                      z_recv.at[f, kind, way], rep, z_minus if way == 0 else z_plus)
+        sent, got, _ = fields[f]
+        return remote(sent.at[kind, way], got.at[kind, way], sem["wide_send" if f == 4 else "slim_send"],
+                      far_recv.at[f, way] if kind == 0 else near_recv.at[f],
+                      rep, z_minus if way == 0 else z_plus)
 
     def far(f, x):
-        zs[f, 0, 0] = x[top].astype(bf16)
-        zs[f, 0, 1] = x[bottom].astype(bf16)
         for way in range(2):
+            fields[f][0][0, way] = x[top if way == 0 else bottom].astype(bf16)
             z_copy(f, 0, way).start()
 
     def near(f, way, x):
-        zs[f, 1, way] = (x[bottom] if way == 0 else x[top]).astype(bf16)
-        kept[f, way] = x[top] if way == 0 else x[bottom]
+        fields[f][0][1, way] = x[bottom if way == 0 else top].astype(bf16)
+        fields[f][2][way] = x[top if way == 0 else bottom]
         z_copy(f, 1, way).start()
 
-    def relay(f, way):
-        z_copy(f, 0, way).wait_recv()
-        zs[f, 2, way] = (kept[f, way] + zr[f, 0, way].astype(f32)).astype(bf16)
-        z_copy(f, 2, way).start()
+    def relay(f):
+        sent, got, mid = fields[f]
+        for way in range(2):
+            z_copy(f, 0, way).wait_recv()
+            sent[2, way] = (mid[way] + got[0, way].astype(f32)).astype(bf16)
+            z_copy(f, 2, way).start()
 
     def arrived(f):
-        for kind in (1, 2):
-            for way in range(2):
-                z_copy(f, kind, way).wait_recv()
-        first = zr[f, 2, 0].astype(f32) + zr[f, 1, 1].astype(f32)
-        last = zr[f, 2, 1].astype(f32) + zr[f, 1, 0].astype(f32)
+        got = fields[f][1]
+        both = got.at[1:3]
+        pltpu.make_async_copy(both, both, near_recv.at[f]).wait()
+        first = got[2, 0].astype(f32) + got[1, 1].astype(f32)
+        last = got[2, 1].astype(f32) + got[1, 0].astype(f32)
         return jnp.concatenate([first, last], axis=0)
 
     def x_first(d):
-        xs0[d] = block(other, d, 0).astype(bf16)
-        x0_copy(d).start()
+        x = block(other, d, 0).astype(bf16)
+        for n in range(2):
+            xs0[n, d] = x[:, n * SLIM : (n + 1) * SLIM]
+            x0_copy(n, d).start()
+
+    def x_sum(n, d):
+        x0_copy(n, d).wait_recv()
+        return own0[d, :, n * SLIM : (n + 1) * SLIM] + xr0[n, d].astype(f32)
 
     def m_copy(src, dst, n, to):
-        return remote(mid_p.at[src], mid_p.at[dst], m_send.at[n], m_recv.at[n], rep, to)
+        return remote(mid_p.at[src], mid_p.at[dst], sem["m_send"], sem["m_x" if n == 0 else "m_z"], rep, to)
 
     m_x = m_copy(0, 1, 0, across_x)
     m_minus = m_copy(2, 3, 1, z_minus)
@@ -447,104 +479,113 @@
     m_two = m_copy(2, 5, 3, a * 4 + z_at(2))
 
     with jax.named_scope("send0"):
-        far(1, field(1, 2))
+        x_first(2)
+        x = block(other, 2, 1)
+        far(2, x[:, :SLIM])
+        far(3, x[:, SLIM:])
     with jax.named_scope("middle"):
         middle = dot(ctx_b[...], od_v[...])
         middle = jnp.where(left[0:32], middle[0:32], pltpu.roll(middle[32:64], 64, axis=1))
         mid_p[0] = middle.astype(bf16)
         m_x.start()
     with jax.named_scope("send1"):
-        x_first(2)
-        far(2, field(2, 2))
         x_first(3)
-        near(1, 0, field(1, 3))
-        near(1, 1, field(1, 1))
+        for way, d in ((0, 3), (1, 1)):
+            x = block(other, d, 1)
+            near(2, way, x[:, :SLIM])
+            near(3, way, x[:, SLIM:])
         x_first(1)
-        near(2, 0, field(2, 3))
-        near(2, 1, field(2, 1))
+        far(4, block(a, 2, 1))
+        near(4, 0, block(a, 3, 1))
+        near(4, 1, block(a, 1, 1))
     with jax.named_scope("send2"):
         x_first(0)
-        own0[0] = field(0, 2)
-        own0[1] = field(0, 3)
-        own0[2] = field(0, 1)
-    with jax.named_scope("relay1"):
-        for way in range(2):
-            relay(1, way)
+        own0[2] = block(a, 2, 0)
+        own0[3] = block(a, 3, 0)
     with jax.named_scope("own"):
-        mine[1] = field(1, 0)
-        mine[0] = field(0, 0)
-        mine[2] = field(2, 0)
+        own0[1] = block(a, 1, 0)
+        mine[1] = block(other, 0, 1)
+    with jax.named_scope("relay2"):
+        relay(2)
+    with jax.named_scope("x_far0"):
+        far(0, x_sum(0, 2))
+    with jax.named_scope("relay3"):
+        relay(3)
+    with jax.named_scope("x_far"):
+        far(1, x_sum(1, 2))
     with jax.named_scope("mid_x"):
-        m_x.wait_recv()
+        wait(mid_p.at[1], "m_x")
         mid_p[2] = (mid_p[0].astype(f32) + mid_p[1].astype(f32)).astype(bf16)
         m_two.start()
         m_minus.start()
         m_plus.start()
-    with jax.named_scope("x_far"):
-        x0_copy(2).wait_recv()
-        far(0, own0[0] + xr0[2].astype(f32))
-    with jax.named_scope("relay2"):
-        for way in range(2):
-            relay(2, way)
-    with jax.named_scope("x_near0"):
-        x0_copy(3).wait_recv()
-        near(0, 0, own0[1] + xr0[3].astype(f32))
+    with jax.named_scope("own2"):
+        wait(uto.at[core, 0:7], "o_recv")
+        uto[core, slot_for(t)] = ug[t, 48:80]
+        o_across.start()
+        mine[0] = block(a, 0, 0)
+        mine[2] = block(a, 0, 1)
+    with jax.named_scope("relay4"):
+        relay(4)
     with jax.named_scope("ou"):
+        wait(uto.at[1 - core], "oo_recv")
         for n in range(TP):
-            e = utl[(2 * n) // TP, (2 * n) % TP, 16:48, :].astype(f32)
-            g = utl[(2 * n) // TP, (2 * n + 1) % TP, 16:48, :].astype(f32)
+            e = uto[(2 * n) // TP, (2 * n) % TP].astype(f32)
+            g = uto[(2 * n) // TP, (2 * n + 1) % TP].astype(f32)
             e_r, g_r = pltpu.roll(e, 64, axis=1), pltpu.roll(g, 64, axis=1)
             ou_v[0:32, n * 128 : (n + 1) * 128] = jnp.where(left[0:32], e, g_r).astype(bf16)
             ou_v[32:64, n * 128 : (n + 1) * 128] = jnp.where(left[0:32], e_r, g).astype(bf16)
-    with jax.named_scope("done1"):
-        xs1[...] = (mine[1] + arrived(1)).astype(bf16)
-        x1_copy.start()
+    with jax.named_scope("x_near0"):
+        for n in range(2):
+            near(n, 0, x_sum(n, 3))
+    with jax.named_scope("done2"):
+        xs1[0] = (mine[1, :, :SLIM] + arrived(2)).astype(bf16)
+        x1_copy(0).start()
+    with jax.named_scope("done3"):
+        xs1[1] = (mine[1, :, SLIM:] + arrived(3)).astype(bf16)
+        x1_copy(1).start()
     with jax.named_scope("x_near1"):
-        x0_copy(1).wait_recv()
-        near(0, 1, own0[2] + xr0[1].astype(f32))
+        for n in range(2):
+            near(n, 1, x_sum(n, 1))
     with jax.named_scope("relay0"):
-        for way in range(2):
-            relay(0, way)
-    with jax.named_scope("done2"):
-        mine[2] = mine[2] + arrived(2)
+        relay(0)
+        relay(1)
     with jax.named_scope("delta"):
-        for copy in (m_minus, m_plus, m_two):
-            copy.wait_recv()
+        wait(mid_p.at[3:6], "m_z")
         middle = mid_p[2].astype(f32)
         for n in range(3, 6):
             middle = middle + mid_p[n].astype(f32)
         middle = jnp.concatenate([middle, pltpu.roll(middle, 64, axis=1)], axis=0)[:, 0:64].astype(bf16)
         delta = adapter_scale * dot(middle, ou_v[...])
+        mine[0] = mine[0] + delta[:, 0:PART]
+        mine[2] = mine[2] + delta[:, PART:]
+    with jax.named_scope("done4"):
+        mine[2] = mine[2] + arrived(4)
+    with jax.named_scope("x0_wait"):
+        for n in range(2):
+            cols = slice(n * SLIM, (n + 1) * SLIM)
+            x0_copy(n, 0).wait_recv()
+            mine[0, :, cols] = mine[0, :, cols] + xr0[n, 0].astype(f32)
+    with jax.named_scope("x1_wait"):
+        for n in range(2):
+            x1_copy(n).wait_recv()
+            cols = slice(n * SLIM, (n + 1) * SLIM)
+            out[:, PART + n * SLIM : PART + (n + 1) * SLIM] = (mine[2, :, cols] + xr1[n].astype(f32)).astype(bf16)
     with jax.named_scope("done0"):
-        x0_copy(0).wait_recv()
-        x = mine[0] + xr0[0].astype(f32) + delta[:, 0:PART]
-        out[:, 0:PART] = (x + arrived(0)).astype(bf16)
-    with jax.named_scope("x1_wait"):
-        x1_copy.wait_recv()
-    out[:, PART:] = (mine[2] + delta[:, PART:] + xr1[...].astype(f32)).astype(bf16)
+        for n in range(2):
+            cols = slice(n * SLIM, (n + 1) * SLIM)
+            out[:, cols] = (mine[0, :, cols] + arrived(n)).astype(bf16)
 
     with jax.named_scope("drain"):
-        for j in range(1, CHIPS):
-            d_copy(j).wait_send()
-            u_copy(j).wait_send()
-        for j in range(CHIPS):
-            across(j).wait_send()
-        t_across.wait_send()
-        l_across.wait_send()
-        for j in range(1, TP):
-            i_copy(j).wait_send()
-            v_copy(j).wait_send()
-            t_copy(j).wait_send()
-            l_copy(j).wait_send()
-        for copy in (m_x, m_minus, m_plus, m_two):
-            copy.wait_send()
-        for d in range(4):
-            x0_copy(d).wait_send()
-        x1_copy.wait_send()
-        for f in range(3):
-            for kind in range(3):
-                for way in range(2):
-                    z_copy(f, kind, way).wait_send()
+        for ref, name in (
+            (dg.at[core, 0:7], "d_send"), (dg.at[core], "across_send"), (ug.at[0:7, 0:32], "u_send"),
+            (ug.at[0:7, 32:48], "e_send"), (ug.at[0:7, 48:80], "w_send"), (ug.at[0:7, 0:32], "t_send"),
+            (ug.at[0:7, 32:48], "l_send"), (ug.at[0:7, 48:80], "o_send"), (ute.at[core], "tt_send"),
+            (utl.at[core], "ll_send"), (uto.at[core], "oo_send"), (inner_p.at[0:7], "i_send"),
+            (inner_v.at[0:7], "v_send"), (mid_p.at[0:4], "m_send"), (xs0, "x0_send"), (xs1, "x1_send"),
+            (hs, "slim_send"), (zs, "wide_send"),
+        ):
+            wait(ref, name)
 
 
 def local(
@@ -579,20 +620,24 @@
             vmem((2, CHIPS, 128, 256), bf16),
             vmem((CHIPS, UROWS, 128), bf16),
             vmem((2, TP, 32, 128), bf16),
-            vmem((2, TP, 48, 128), bf16),
+            vmem((2, TP, 16, 128), bf16),
+            vmem((2, TP, 32, 128), bf16),
+            vmem((TP, 32, 128), bf16),
             vmem((TP, SEQS, 128), bf16),
-            vmem((TP, 32, 128), bf16),
             vmem((RANK, OUTC), bf16),
             vmem((QCOLS, 128), bf16),
             vmem((6, 32, 128), bf16),
-            vmem((4, SEQS, PART), bf16),
-            vmem((4, SEQS, PART), bf16),
-            vmem((3, 3, 2, 32, PART), bf16),
-            vmem((3, 3, 2, 32, PART), bf16),
-            vmem((SEQS, PART), bf16),
-            vmem((SEQS, PART), bf16),
-            vmem((3, 2, 32, PART), f32),
-            vmem((3, SEQS, PART), f32),
+            vmem((2, 4, SEQS, SLIM), bf16),
+            vmem((2, 4, SEQS, SLIM), bf16),
+            vmem((3, 2, 32, PART), bf16),
+            vmem((3, 2, 32, PART), bf16),
+            vmem((4, 3, 2, 32, SLIM), bf16),
+            vmem((4, 3, 2, 32, SLIM), bf16),
+            vmem((2, SEQS, SLIM), bf16),
+            vmem((2, SEQS, SLIM), bf16),
+            vmem((2, 32, PART), f32),
+            vmem((4, 2, 32, SLIM), f32),
+            vmem((4, SEQS, PART), f32),
             vmem((3, SEQS, PART), f32),
             vmem((SEQS, QCOLS), f32),
             vmem((SEQS, HEAD), f32),
@@ -601,12 +646,10 @@
             vmem((SEQS * 8, HEAD), f32),
             vmem((SEQS * 8, HEAD), f32),
             vmem((SEQS * 8, HEAD), f32),
+            vmem((SEQS * 8, HEAD), f32),
             vmem((SEQS, QCOLS), bf16),
-            dma((4,)), dma((CHUNKS,)), dma((CHUNKS,)), dma((7,)),
-            dma((CHIPS,)), dma((CHIPS,)), dma((CHIPS,)), dma((CHIPS,)), dma((CHIPS,)), dma((CHIPS,)),
-            dma((TP,)), dma((TP,)), dma((2,)), dma((TP,)), dma((TP,)), dma((2,)),
-            dma((TP,)), dma((TP,)), dma((TP,)), dma((TP,)), dma((4,)), dma((4,)),
-            dma((4,)), dma((4,)), dma((2,)), dma((3, 3, 2)), dma((3, 3, 2)),
+            dma((4,)), dma((CHUNKS,)), dma((7,)),
+            dma((CHIPS,)), dma((2, 4)), dma((2,)), dma((5, 2)), dma((5,)), dma((32,)),
         ],
         compiler_params=pltpu.CompilerParams(
             collective_id=0, has_side_effects=True, vmem_limit_bytes=48 * 1024 * 1024),

time: 36.2 us -> 33.4 us (0.923)
  Pallas kernels: 35.5 us -> 32.7 us
    pallas_call x1, Pallas kernels: 35.5 us -> 32.7 us  [local(): pl.pallas_call(kernel, out_shape=jax.ShapeDtypeStruct((SEQS, OUTC), bf16)...]
where the time goes in v4:
time: 33.4 us; the launch traced here: 33.3 us
  Pallas kernels  32.7 us (98%)
  local copies, waits for them, and re-layouts  0.66 us (2%)
    pallas_call x1, Pallas kernels, local(): pl.pallas_call(kernel, out_shape=jax.ShapeDtypeStruct((SEQS, OUTC), bf16)...  32.7 us

profile of v4, /device:TPU:0, one launch (start us, length us, event | category | flops | bytes accessed | tf_op | source)
XLA Modules:
  0.0 33.3 jit_solution(7933521800467905058)
XLA Ops:
  0.0 32.7 %shard_map.127 = bf16[64,1024]{1,0:T(8,128)(2,1)S(1)} custom-call(bf16[64,8192]{1,0:T(8,128)(2,1)} %hidden.1, bf16[8192]{0:T(1024)(128)(2,1)} %gain.1, bf16[8192,512]{1,0:T(8,128)(2,1)} %wq.1, bf16[2,8192,128]{2,1,0:T(8,128)(2,1)} %wkv.1, bf16[512,8192]{1,0:T(8,128)(2,1)} %wo.1, bf16[3,64,64]{2,1,0:T(8,128)(2,1)} %down.1, bf16[32,64]{1,0:T(8,128)(2,1)} %bitcast.2, ...), custom_call_target="tpu_custom_call" | custom-call | flops 3000000000 | bytes 27262976 | tf_op jit(solution)/shard_map/pallas_call | solution.py:599
  32.7 0.7 %copy.15 = bf16[64,1024]{1,0:T(8,128)(2,1)} copy(bf16[64,1024]{1,0:T(8,128)(2,1)S(1)} %shard_map.127) | data formatting | bytes 262144

commit v5 on v4

--- a/solution.py
+++ b/solution.py
@@ -27,6 +27,11 @@
 DROWS = 96
 UROWS = 80
 GROUP = 32
+SENT_ROWS = (
+    7 * DROWS + 8 * DROWS + 2 * 7 * UROWS + 8 * UROWS + 7 * 32 + 7 * 64 + 4 * 32
+    + 1024 + 256 + 1536 + 768
+)
+SENT_BYTES = SENT_ROWS * 256
 PART = 512
 SLIM = 256
 
@@ -50,14 +55,12 @@
     out,
     hid_v, nrm_v, wq_v, wkv_v, wo_v, k_v, v_v,
     down_v, qup_v, kvup_v, odown_v, oup_v, gain_v, len_v,
-    dg, w2, ug, ute, utl, uto, inner_p, inner_v, ou_v, od_v, mid_p,
+    dg, d2, own_x, own_y, ug, ute, utl, uto, inner_p, inner_v, ou_v, od_v, mid_p,
     xs0, xr0, zs, zr, hs, hr, xs1, xr1, kept, kept_h, own0, mine, qacc, kacc, vacc, q_s, max_s, sum_s, ctx_s, len_s, ctx_b,
     load_sem, wq_sem, small_sem,
     d_recv, x0_recv, x1_recv, far_recv, near_recv, sems,
 ):
-    names = ("d_send across_send across_recv u_send u_recv e_send e_recv w_send w_recv t_send t_recv "
-             "tt_send tt_recv l_send l_recv ll_send ll_recv o_send o_recv oo_send oo_recv i_send i_recv "
-             "v_send v_recv m_send m_x m_z x0_send x1_send slim_send wide_send").split()
+    names = ("send", "across", "d2", "across2", "u", "e", "w", "t", "tt", "l", "ll", "o", "oo", "i", "v", "m_x", "m_z")
     sem = {name: sems.at[n] for n, name in enumerate(names)}
 
     def wait(ref, name):
@@ -82,8 +85,11 @@
 
     far_first = (4, 3, 5, 1, 7, 2, 6)
 
+    farthest = ((1, 2), (0, 2), (1, 1), (1, 3), (0, 1), (0, 3), (1, 0))
+
     def tp_at(j):
-        return lax.rem(t + j, TP)
+        da, dk = farthest[j - 1]
+        return lax.rem(a + da, 2) * 4 + lax.rem(k + dk, 4)
 
     def z_at(d):
         return lax.rem(k + d, 4)
@@ -136,8 +142,8 @@
     low, high = at_lanes(0, RANK), at_lanes(64, RANK)
     with jax.named_scope("pack"):
         small[0].wait()
-        dg[core, chip, 0:64, :] = (dot(down_v[0], low) + dot(down_v[1], high)).astype(bf16)
-        dg[core, chip, 64:96, :] = (dot(down_v[2, 0:32, :], low) + dot(down_v[2, 32:64, :], high)).astype(bf16)
+        dg[core, chip] = (dot(down_v[0], low) + dot(down_v[1], high)).astype(bf16)
+        d2[core, chip] = (dot(down_v[2, 0:32, :], low) + dot(down_v[2, 32:64, :], high)).astype(bf16)
         for copy in small[1:]:
             copy.wait()
         ug[chip, 0:16, :] = (dot(qup_v[0:16, :], low) + dot(qup_v[16:32, :], high)).astype(bf16)
@@ -146,37 +152,6 @@
         ug[chip, 32:48, :] = (dot(odown_v[0:16, :], low) + dot(odown_v[16:32, :], high)).astype(bf16)
         ug[chip, 48:80, :] = (dot(oup_v[0:32, :], low) + dot(oup_v[32:64, :], high)).astype(bf16)
 
-    with jax.named_scope("barrier_wait"):
-        pl.semaphore_wait(barrier, CHIPS + TP - 1)
-
-    def d_copy(j):
-        return remote(dg.at[core, chip], dg.at[core, chip], sem["d_send"], d_recv.at[j],
-                      *gather_peer(j))
-
-    def u_copy(j):
-        piece = ug.at[chip, 0:32]
-        return remote(piece, piece, sem["u_send"], sem["u_recv"], *gather_peer(j))
-
-    def e_copy(j):
-        piece = ug.at[chip, 32:48]
-        return remote(piece, piece, sem["e_send"], sem["e_recv"], *gather_peer(j))
-
-    def w_copy(j):
-        piece = ug.at[chip, 48:80]
-        return remote(piece, piece, sem["w_send"], sem["w_recv"], *gather_peer(j))
-
-    def across(j):
-        q = lax.rem(chip + CHIPS - j, CHIPS)
-        return remote(dg.at[core, q], dg.at[core, q], sem["across_send"], sem["across_recv"], partner, t)
-
-    for j in far_first:
-        u_copy(j).start()
-    for j in far_first:
-        d_copy(j).start()
-    across(0).start()
-    for j in far_first:
-        e_copy(j).start()
-
     with jax.named_scope("hid_wait"):
         hid_copy.wait()
 
@@ -201,7 +176,42 @@
 
         lax.fori_loop(0, CHUNKS, normalise, 0)
 
-    w2[...] = jnp.zeros_like(w2)
+    with jax.named_scope("barrier_wait"):
+        pl.semaphore_wait(barrier, CHIPS + TP - 1)
+
+    def d_copy(j):
+        return remote(dg.at[core, chip], dg.at[core, chip], sem["send"], d_recv.at[j],
+                      *gather_peer(j))
+
+    def u_copy(j):
+        piece = ug.at[chip, 0:32]
+        return remote(piece, piece, sem["send"], sem["u"], *gather_peer(j))
+
+    def e_copy(j):
+        piece = ug.at[chip, 32:48]
+        return remote(piece, piece, sem["send"], sem["e"], *gather_peer(j))
+
+    def w_copy(j):
+        piece = ug.at[chip, 48:80]
+        return remote(piece, piece, sem["send"], sem["w"], *gather_peer(j))
+
+    def across(j):
+        q = lax.rem(chip + CHIPS - j, CHIPS)
+        return remote(dg.at[core, q], dg.at[core, q], sem["send"], sem["across"], partner, t)
+
+    def d2_copy(j):
+        return remote(d2.at[core, chip], d2.at[core, chip], sem["send"], sem["d2"], *gather_peer(j))
+
+    for j in far_first:
+        u_copy(j).start()
+    for j in far_first:
+        d_copy(j).start()
+    across(0).start()
+    for j in far_first:
+        d2_copy(j).start()
+    for j in far_first:
+        e_copy(j).start()
+
     qacc[...] = jnp.zeros_like(qacc)
     kacc[...] = jnp.zeros_like(kacc)
     vacc[...] = jnp.zeros_like(vacc)
@@ -237,6 +247,27 @@
         cosine = jnp.cos(angles)
         sine = jnp.where(left, -jnp.sin(angles), jnp.sin(angles))
 
+    with jax.named_scope("own_features"):
+        for c in range(2):
+            parts = []
+            for q in range(CHIPS):
+                owner = lax.rem(t + 4 * lax.rem(chip + q, 2), TP)
+                at = pl.multiple_of((2 * q + c) * QCOLS + (owner // 2) * 128, 128)
+                x = nrm_v[:, pl.ds(at, 128)].astype(f32)
+                parts.append(jnp.where(left, jnp.where(t % 2 == 0, x, pltpu.roll(x, 64, axis=1)), 0.0))
+            for n in range(CHIPS // 2):
+                x = parts[2 * n] + pltpu.roll(parts[2 * n + 1], 64, axis=1)
+                own_x[c, :, n * 128 : (n + 1) * 128] = x.astype(bf16)
+            for n in range(CHIPS // 4):
+                first, last = 0.0, 0.0
+                for m in range(4):
+                    x = parts[4 * n + m]
+                    x1, x2 = jnp.where(lane < 32, x, 0.0), jnp.where(lane < 32, 0.0, x)
+                    first = first + (pltpu.roll(x1, 32 * m, axis=1) if m else x1)
+                    last = last + (pltpu.roll(x2, (32 * m + 96) % 128, axis=1) if m != 1 else x2)
+                own_y[c, 0:64, n * 128 : (n + 1) * 128] = first.astype(bf16)
+                own_y[c, 64:128, n * 128 : (n + 1) * 128] = last.astype(bf16)
+
     def rotate(x):
         return x * cosine + pltpu.roll(x, 64, axis=1) * sine
 
@@ -245,18 +276,18 @@
 
     def t_copy(j):
         to = tp_at(j)
-        return remote(ug.at[to, 0:32], ute.at[core, slot_for(to)], sem["t_send"], sem["t_recv"], rep, to)
+        return remote(ug.at[to, 0:32], ute.at[core, slot_for(to)], sem["send"], sem["t"], rep, to)
 
     def l_copy(j):
         to = tp_at(j)
-        return remote(ug.at[to, 32:48], utl.at[core, slot_for(to)], sem["l_send"], sem["l_recv"], rep, to)
+        return remote(ug.at[to, 32:48], utl.at[core, slot_for(to)], sem["send"], sem["l"], rep, to)
 
     def o_copy(j):
         to = tp_at(j)
-        return remote(ug.at[to, 48:80], uto.at[core, slot_for(to)], sem["o_send"], sem["o_recv"], rep, to)
+        return remote(ug.at[to, 48:80], uto.at[core, slot_for(to)], sem["send"], sem["o"], rep, to)
 
     with jax.named_scope("u_wait"):
-        wait(ug.at[0:7, 0:32], "u_recv")
+        wait(ug.at[0:7, 0:32], "u")
         for j in range(1, TP):
             t_copy(j).start()
     with jax.named_scope("d_wait"):
@@ -266,59 +297,62 @@
     for j in far_first:
         w_copy(j).start()
 
-    half = pl.multiple_of((t % 2) * 64, 64)
-
-    def spread(c):
-        for q in range(CHIPS):
-            w2[c, q, pl.ds(half, 64), 0:128] = dg[c, q, 0:64, :]
-            tail = dg[c, q, 64:96, :].astype(f32)
-            both = jnp.concatenate([tail, pltpu.roll(tail, 64, axis=1)], axis=0)
-            w2[c, q, pl.ds(half, 64), 128:256] = both.astype(bf16)
-
     def features(c):
-        total = jnp.zeros((SEQS, 256), f32)
-        for j in range(CHIPS):
-            at = (chip_at(j) * 2 + c) * QCOLS + (tp_of(j) // 2) * 128
-            total = total + dot(nrm_v[:, pl.ds(pl.multiple_of(at, 128), 128)], w2[c, chip_at(j)])
-        return total
+        return dot(own_x[c], dg[c].reshape(CHIPS * 64, 128))
+
+    def value_features(c):
+        return dot(own_y[c], d2[c].reshape(CHIPS * 32, 128))
+
+    def pass_values():
+        wait(d2.at[core, 0:7], "d2")
+        remote(d2.at[core], d2.at[core], sem["send"], sem["across2"], partner, t).start()
+
+    @pl.when(core == 1)
+    def _():
+        pass_values()
 
     with jax.named_scope("inner_own"):
-        spread(core)
         partial = features(core)
 
     with jax.named_scope("across_wait"):
-        wait(dg.at[1 - core], "across_recv")
+        wait(dg.at[1 - core], "across")
     with jax.named_scope("inner_other"):
-        spread(1 - core)
         partial = partial + features(1 - core)
-        first, tail = partial[:, 0:128], partial[:, 128:256]
-        packed = jnp.where(left[0:32], first[0:32], pltpu.roll(first[32:64], 64, axis=1))
+        packed = jnp.where(left[0:32], partial[0:32], pltpu.roll(partial[32:64], 64, axis=1))
         inner_p[t] = packed.astype(bf16)
-        inner_v[t] = jnp.where(left, tail, first).astype(bf16)
 
     def i_copy(j):
-        return remote(inner_p.at[t], inner_p.at[t], sem["i_send"], sem["i_recv"], rep, tp_at(j))
+        return remote(inner_p.at[t], inner_p.at[t], sem["send"], sem["i"], rep, tp_at(j))
 
     def v_copy(j):
-        return remote(inner_v.at[t], inner_v.at[t], sem["v_send"], sem["v_recv"], rep, tp_at(j))
+        return remote(inner_v.at[t], inner_v.at[t], sem["send"], sem["v"], rep, tp_at(j))
 
     for j in range(1, TP):
         i_copy(j).start()
+    with jax.named_scope("d2_wait"):
+
+        @pl.when(core == 0)
+        def _():
+            pass_values()
+
+    with jax.named_scope("w_wait"):
+        wait(ug.at[0:7, 32:48], "e")
+        for j in range(1, TP):
+            l_copy(j).start()
+        wait(d2.at[1 - core], "across2")
+        x = value_features(core) + value_features(1 - core)
+        inner_v[t] = jnp.where(left, x[0:64] + pltpu.roll(x[64:128], 64, axis=1), partial).astype(bf16)
     for j in range(1, TP):
         v_copy(j).start()
-    with jax.named_scope("w_wait"):
-        wait(ug.at[0:7, 32:48], "e_recv")
-    for j in range(1, TP):
-        l_copy(j).start()
     ute[core, slot_for(t)] = ug[t, 0:32]
     utl[core, slot_for(t)] = ug[t, 32:48]
 
     with jax.named_scope("t_wait"):
-        wait(ute.at[core, 0:7], "t_recv")
-    t_across = remote(ute.at[core], ute.at[core], sem["tt_send"], sem["tt_recv"], partner, t)
+        wait(ute.at[core, 0:7], "t")
+    t_across = remote(ute.at[core], ute.at[core], sem["send"], sem["tt"], partner, t)
     t_across.start()
     with jax.named_scope("up_wait"):
-        wait(ute.at[1 - core], "tt_recv")
+        wait(ute.at[1 - core], "tt")
     with jax.named_scope("unpack"):
         rows = []
         for n in range(2 * TP):
@@ -329,7 +363,7 @@
             [ute[n // TP, n % TP, 16:32, :].astype(f32)[0:8] for n in range(2 * TP)], axis=0).astype(bf16)
 
     with jax.named_scope("i_wait"):
-        wait(inner_p.at[0:7], "i_recv")
+        wait(inner_p.at[0:7], "i")
     score_scale = 1.0 / math.sqrt(HEAD)
     with jax.named_scope("queries"):
         inner = inner_p[0].astype(f32)
@@ -351,8 +385,8 @@
     wide = 8 * GROUP
     position = lax.broadcasted_iota(jnp.int32, (wide, 128), 1).astype(f32)
 
-    def attend(g, carry):
-        rows = pl.ds(pl.multiple_of(g * wide, wide), wide)
+    def attend(g):
+        rows = pl.ds(g * wide, wide)
         q_rows = q_s[rows, :].astype(bf16)
         scores = []
         for s in range(GROUP):
@@ -370,28 +404,23 @@
             dot(probs[s * 8 : (s + 1) * 8], v_v[g * GROUP + s, 0]) for s in range(GROUP)
         ]
         ctx_s[rows, :] = jnp.concatenate(parts, axis=0)
-        return carry
 
     with jax.named_scope("attend"):
-        lax.fori_loop(0, SEQS // GROUP // 2, attend, 0)
+        attend(0)
     with jax.named_scope("late_wait"):
-        wait(inner_v.at[0:7], "v_recv")
-        wait(utl.at[core, 0:7], "l_recv")
-    l_across = remote(utl.at[core], utl.at[core], sem["ll_send"], sem["ll_recv"], partner, t)
+        wait(utl.at[core, 0:7], "l")
+    l_across = remote(utl.at[core], utl.at[core], sem["send"], sem["ll"], partner, t)
     l_across.start()
     with jax.named_scope("o_start"):
-        wait(ug.at[0:7, 48:80], "w_recv")
+        wait(ug.at[0:7, 48:80], "w")
         for j in range(1, TP):
             o_copy(j).start()
     with jax.named_scope("attend2"):
-        lax.fori_loop(SEQS // GROUP // 2, SEQS // GROUP, attend, 0)
-
+        attend(1)
+
+    with jax.named_scope("v_wait"):
+        wait(inner_v.at[0:7], "v")
     with jax.named_scope("context"):
-        wait(utl.at[1 - core], "ll_recv")
-        for n in range(2 * TP):
-            e = utl[n // TP, n % TP].astype(f32)
-            e = jnp.concatenate([e, pltpu.roll(e, 64, axis=1)], axis=0)
-            od_v[n * 32 : (n + 1) * 32, :] = e.astype(bf16)
         inner = inner_v[0].astype(f32)
         for n in range(1, TP):
             inner = inner + inner_v[n].astype(f32)
@@ -411,27 +440,27 @@
 
     with jax.named_scope("wo_wait"):
         wo_copy.wait()
-    o_across = remote(uto.at[core], uto.at[core], sem["oo_send"], sem["oo_recv"], partner, t)
+    o_across = remote(uto.at[core], uto.at[core], sem["send"], sem["oo"], partner, t)
 
     z_minus, z_plus = a * 4 + z_at(3), a * 4 + z_at(1)
     across_x = other * 4 + k
     top, bottom = slice(0, 32), slice(32, 64)
 
-    def block(a_to, d, part):
-        at = (a_to * 4 + z_at(d)) * OUTC + part * PART
-        return dot(ctx_b[...], wo_v[:, pl.ds(pl.multiple_of(at, PART), PART)])
+    def block(a_to, d):
+        at = (a_to * 4 + z_at(d)) * OUTC
+        return dot(ctx_b[...], wo_v[:, pl.ds(pl.multiple_of(at, OUTC), OUTC)])
 
     def x0_copy(n, d):
-        return remote(xs0.at[n, d], xr0.at[n, d], sem["x0_send"], x0_recv.at[n, d], rep, across_x)
+        return remote(xs0.at[n, d], xr0.at[n, d], sem["send"], x0_recv.at[n, d], rep, across_x)
 
     def x1_copy(n):
-        return remote(xs1.at[n], xr1.at[n], sem["x1_send"], x1_recv.at[n], rep, across_x)
+        return remote(xs1.at[n], xr1.at[n], sem["send"], x1_recv.at[n], rep, across_x)
 
     fields = [(hs.at[f], hr.at[f], kept_h.at[f]) for f in range(4)] + [(zs, zr, kept)]
 
     def z_copy(f, kind, way):
         sent, got, _ = fields[f]
-        return remote(sent.at[kind, way], got.at[kind, way], sem["wide_send" if f == 4 else "slim_send"],
+        return remote(sent.at[kind, way], got.at[kind, way], sem["send"],
                       far_recv.at[f, way] if kind == 0 else near_recv.at[f],
                       rep, z_minus if way == 0 else z_plus)
 
@@ -460,18 +489,27 @@
         last = got[2, 1].astype(f32) + got[1, 0].astype(f32)
         return jnp.concatenate([first, last], axis=0)
 
-    def x_first(d):
-        x = block(other, d, 0).astype(bf16)
+    def x_first(d, x):
         for n in range(2):
-            xs0[n, d] = x[:, n * SLIM : (n + 1) * SLIM]
+            xs0[n, d] = x[:, n * SLIM : (n + 1) * SLIM].astype(bf16)
             x0_copy(n, d).start()
+
+    def other_far(x):
+        x_first(2, x)
+        far(2, x[:, PART : PART + SLIM])
+        far(3, x[:, PART + SLIM :])
+
+    def other_near(d, way, x):
+        x_first(d, x)
+        near(2, way, x[:, PART : PART + SLIM])
+        near(3, way, x[:, PART + SLIM :])
 
     def x_sum(n, d):
         x0_copy(n, d).wait_recv()
         return own0[d, :, n * SLIM : (n + 1) * SLIM] + xr0[n, d].astype(f32)
 
     def m_copy(src, dst, n, to):
-        return remote(mid_p.at[src], mid_p.at[dst], sem["m_send"], sem["m_x" if n == 0 else "m_z"], rep, to)
+        return remote(mid_p.at[src], mid_p.at[dst], sem["send"], sem["m_x" if n == 0 else "m_z"], rep, to)
 
     m_x = m_copy(0, 1, 0, across_x)
     m_minus = m_copy(2, 3, 1, z_minus)
@@ -479,32 +517,31 @@
     m_two = m_copy(2, 5, 3, a * 4 + z_at(2))
 
     with jax.named_scope("send0"):
-        x_first(2)
-        x = block(other, 2, 1)
-        far(2, x[:, :SLIM])
-        far(3, x[:, SLIM:])
+        other_far(block(other, 2))
     with jax.named_scope("middle"):
+        wait(utl.at[1 - core], "ll")
+        for n in range(2 * TP):
+            e = utl[n // TP, n % TP].astype(f32)
+            e = jnp.concatenate([e, pltpu.roll(e, 64, axis=1)], axis=0)
+            od_v[n * 32 : (n + 1) * 32, :] = e.astype(bf16)
         middle = dot(ctx_b[...], od_v[...])
         middle = jnp.where(left[0:32], middle[0:32], pltpu.roll(middle[32:64], 64, axis=1))
         mid_p[0] = middle.astype(bf16)
         m_x.start()
     with jax.named_scope("send1"):
-        x_first(3)
+        other_near(3, 0, block(other, 3))
+        other_near(1, 1, block(other, 1))
+        x = block(a, 2)
+        far(4, x[:, PART:])
+        own0[2] = x[:, :PART]
         for way, d in ((0, 3), (1, 1)):
-            x = block(other, d, 1)
-            near(2, way, x[:, :SLIM])
-            near(3, way, x[:, SLIM:])
-        x_first(1)
-        far(4, block(a, 2, 1))
-        near(4, 0, block(a, 3, 1))
-        near(4, 1, block(a, 1, 1))
+            x = block(a, d)
+            near(4, way, x[:, PART:])
+            own0[d] = x[:, :PART]
     with jax.named_scope("send2"):
-        x_first(0)
-        own0[2] = block(a, 2, 0)
-        own0[3] = block(a, 3, 0)
-    with jax.named_scope("own"):
-        own0[1] = block(a, 1, 0)
-        mine[1] = block(other, 0, 1)
+        x = block(other, 0)
+        x_first(0, x)
+        mine[1] = x[:, PART:]
     with jax.named_scope("relay2"):
         relay(2)
     with jax.named_scope("x_far0"):
@@ -520,15 +557,16 @@
         m_minus.start()
         m_plus.start()
     with jax.named_scope("own2"):
-        wait(uto.at[core, 0:7], "o_recv")
+        wait(uto.at[core, 0:7], "o")
         uto[core, slot_for(t)] = ug[t, 48:80]
         o_across.start()
-        mine[0] = block(a, 0, 0)
-        mine[2] = block(a, 0, 1)
+        x = block(a, 0)
+        mine[0] = x[:, :PART]
+        mine[2] = x[:, PART:]
     with jax.named_scope("relay4"):
         relay(4)
     with jax.named_scope("ou"):
-        wait(uto.at[1 - core], "oo_recv")
+        wait(uto.at[1 - core], "oo")
         for n in range(TP):
             e = uto[(2 * n) // TP, (2 * n) % TP].astype(f32)
             g = uto[(2 * n) // TP, (2 * n + 1) % TP].astype(f32)
@@ -577,15 +615,7 @@
             out[:, cols] = (mine[0, :, cols] + arrived(n)).astype(bf16)
 
     with jax.named_scope("drain"):
-        for ref, name in (
-            (dg.at[core, 0:7], "d_send"), (dg.at[core], "across_send"), (ug.at[0:7, 0:32], "u_send"),
-            (ug.at[0:7, 32:48], "e_send"), (ug.at[0:7, 48:80], "w_send"), (ug.at[0:7, 0:32], "t_send"),
-            (ug.at[0:7, 32:48], "l_send"), (ug.at[0:7, 48:80], "o_send"), (ute.at[core], "tt_send"),
-            (utl.at[core], "ll_send"), (uto.at[core], "oo_send"), (inner_p.at[0:7], "i_send"),
-            (inner_v.at[0:7], "v_send"), (mid_p.at[0:4], "m_send"), (xs0, "x0_send"), (xs1, "x1_send"),
-            (hs, "slim_send"), (zs, "wide_send"),
-        ):
-            wait(ref, name)
+        wait(wq_v.at[0 : SENT_BYTES // 1024], "send")
 
 
 def local(
@@ -616,8 +646,10 @@
             vmem((RANK, 64), bf16),
             vmem((FEATURES,), bf16),
             vmem((SEQS,), jnp.int32),
-            vmem((2, CHIPS, DROWS, 128), bf16),
-            vmem((2, CHIPS, 128, 256), bf16),
+            vmem((2, CHIPS, 64, 128), bf16),
+            vmem((2, CHIPS, 32, 128), bf16),
+            vmem((2, SEQS, CHIPS * 64), bf16),
+            vmem((2, 2 * SEQS, CHIPS * 32), bf16),
             vmem((CHIPS, UROWS, 128), bf16),
             vmem((2, TP, 32, 128), bf16),
             vmem((2, TP, 16, 128), bf16),
@@ -649,7 +681,7 @@
             vmem((SEQS * 8, HEAD), f32),
             vmem((SEQS, QCOLS), bf16),
             dma((4,)), dma((CHUNKS,)), dma((7,)),
-            dma((CHIPS,)), dma((2, 4)), dma((2,)), dma((5, 2)), dma((5,)), dma((32,)),
+            dma((CHIPS,)), dma((2, 4)), dma((2,)), dma((5, 2)), dma((5,)), dma((17,)),
         ],
         compiler_params=pltpu.CompilerParams(
             collective_id=0, has_side_effects=True, vmem_limit_bytes=48 * 1024 * 1024),

time: 33.4 us -> 32.5 us (0.973)
  Pallas kernels: 32.7 us -> 31.7 us
    pallas_call x1, Pallas kernels: 32.7 us -> 31.7 us  [local(): pl.pallas_call(kernel, out_shape=jax.ShapeDtypeStruct((SEQS, OUTC), bf16)...]
where the time goes in v5:
time: 32.5 us; the launch traced here: 32.4 us
  Pallas kernels  31.7 us (98%)
  local copies, waits for them, and re-layouts  0.66 us (2%)
    pallas_call x1, Pallas kernels, local(): pl.pallas_call(kernel, out_shape=jax.ShapeDtypeStruct((SEQS, OUTC), bf16)...  31.7 us
    unnamed x1, local copies, waits for them, and re-layouts  0.66 us

profile of v5, /device:TPU:0, one launch (start us, length us, event | category | flops | bytes accessed | tf_op | source)
XLA Modules:
  0.0 32.4 jit_solution(9553618899331058799)
XLA Ops:
  0.0 31.7 %shard_map.127 = bf16[64,1024]{1,0:T(8,128)(2,1)S(1)} custom-call(bf16[64,8192]{1,0:T(8,128)(2,1)} %hidden.1, bf16[8192]{0:T(1024)(128)(2,1)} %gain.1, bf16[8192,512]{1,0:T(8,128)(2,1)} %wq.1, bf16[2,8192,128]{2,1,0:T(8,128)(2,1)} %wkv.1, bf16[512,8192]{1,0:T(8,128)(2,1)} %wo.1, bf16[3,64,64]{2,1,0:T(8,128)(2,1)} %down.1, bf16[32,64]{1,0:T(8,128)(2,1)} %bitcast.2, ...), custom_call_target="tpu_custom_call" | custom-call | flops 3000000000 | bytes 27262976 | tf_op jit(solution)/shard_map/pallas_call | solution.py:629
  31.7 0.7 %copy.15 = bf16[64,1024]{1,0:T(8,128)(2,1)} copy(bf16[64,1024]{1,0:T(8,128)(2,1)S(1)} %shard_map.127) | data formatting | bytes 262144

commit v6 on v5

--- a/solution.py
+++ b/solution.py
@@ -26,14 +26,15 @@
 CHUNK = FEATURES // CHUNKS
 DROWS = 96
 UROWS = 80
+WIDTHS = (256, 256, 256, 256, 512)
+STARTS = (0, 256, 512, 768, 512)
+PART = 512
 GROUP = 32
 SENT_ROWS = (
     7 * DROWS + 8 * DROWS + 2 * 7 * UROWS + 8 * UROWS + 7 * 32 + 7 * 64 + 4 * 32
-    + 1024 + 256 + 1536 + 768
+    + (4 * SEQS * PART + SEQS * (OUTC - PART) + 6 * 32 * sum(WIDTHS)) // 128
 )
 SENT_BYTES = SENT_ROWS * 256
-PART = 512
-SLIM = 256
 
 
 def dot(a, b):
@@ -56,7 +57,7 @@
     hid_v, nrm_v, wq_v, wkv_v, wo_v, k_v, v_v,
     down_v, qup_v, kvup_v, odown_v, oup_v, gain_v, len_v,
     dg, d2, own_x, own_y, ug, ute, utl, uto, inner_p, inner_v, ou_v, od_v, mid_p,
-    xs0, xr0, zs, zr, hs, hr, xs1, xr1, kept, kept_h, own0, mine, qacc, kacc, vacc, q_s, max_s, sum_s, ctx_s, len_s, ctx_b,
+    xs0, xr0, zs, zr, xs1, xr1, kept, own0, mine_a, mine_b, qacc, kacc, vacc, q_s, max_s, sum_s, ctx_s, len_s, ctx_b,
     load_sem, wq_sem, small_sem,
     d_recv, x0_recv, x1_recv, far_recv, near_recv, sems,
 ):
@@ -451,38 +452,37 @@
         return dot(ctx_b[...], wo_v[:, pl.ds(pl.multiple_of(at, OUTC), OUTC)])
 
     def x0_copy(n, d):
-        return remote(xs0.at[n, d], xr0.at[n, d], sem["send"], x0_recv.at[n, d], rep, across_x)
+        return remote(xs0[n].at[d], xr0[n].at[d], sem["send"], x0_recv.at[n, d], rep, across_x)
 
     def x1_copy(n):
-        return remote(xs1.at[n], xr1.at[n], sem["send"], x1_recv.at[n], rep, across_x)
-
-    fields = [(hs.at[f], hr.at[f], kept_h.at[f]) for f in range(4)] + [(zs, zr, kept)]
+        return remote(xs1[n], xr1[n], sem["send"], x1_recv.at[n], rep, across_x)
+
+    def columns(f):
+        return slice(STARTS[f], STARTS[f] + WIDTHS[f])
 
     def z_copy(f, kind, way):
-        sent, got, _ = fields[f]
-        return remote(sent.at[kind, way], got.at[kind, way], sem["send"],
+        return remote(zs[f].at[kind, way], zr[f].at[kind, way], sem["send"],
                       far_recv.at[f, way] if kind == 0 else near_recv.at[f],
                       rep, z_minus if way == 0 else z_plus)
 
     def far(f, x):
         for way in range(2):
-            fields[f][0][0, way] = x[top if way == 0 else bottom].astype(bf16)
+            zs[f][0, way] = x[top if way == 0 else bottom].astype(bf16)
             z_copy(f, 0, way).start()
 
     def near(f, way, x):
-        fields[f][0][1, way] = x[bottom if way == 0 else top].astype(bf16)
-        fields[f][2][way] = x[top if way == 0 else bottom]
+        zs[f][1, way] = x[bottom if way == 0 else top].astype(bf16)
+        kept[f][way] = x[top if way == 0 else bottom]
         z_copy(f, 1, way).start()
 
     def relay(f):
-        sent, got, mid = fields[f]
         for way in range(2):
             z_copy(f, 0, way).wait_recv()
-            sent[2, way] = (mid[way] + got[0, way].astype(f32)).astype(bf16)
+            zs[f][2, way] = (kept[f][way] + zr[f][0, way].astype(f32)).astype(bf16)
             z_copy(f, 2, way).start()
 
     def arrived(f):
-        got = fields[f][1]
+        got = zr[f]
         both = got.at[1:3]
         pltpu.make_async_copy(both, both, near_recv.at[f]).wait()
         first = got[2, 0].astype(f32) + got[1, 1].astype(f32)
@@ -491,22 +491,22 @@
 
     def x_first(d, x):
         for n in range(2):
-            xs0[n, d] = x[:, n * SLIM : (n + 1) * SLIM].astype(bf16)
+            xs0[n][d] = x[:, columns(n)].astype(bf16)
             x0_copy(n, d).start()
 
     def other_far(x):
         x_first(2, x)
-        far(2, x[:, PART : PART + SLIM])
-        far(3, x[:, PART + SLIM :])
+        far(2, x[:, columns(2)])
+        far(3, x[:, columns(3)])
 
     def other_near(d, way, x):
         x_first(d, x)
-        near(2, way, x[:, PART : PART + SLIM])
-        near(3, way, x[:, PART + SLIM :])
+        near(2, way, x[:, columns(2)])
+        near(3, way, x[:, columns(3)])
 
     def x_sum(n, d):
         x0_copy(n, d).wait_recv()
-        return own0[d, :, n * SLIM : (n + 1) * SLIM] + xr0[n, d].astype(f32)
+        return own0[d, :, columns(n)] + xr0[n][d].astype(f32)
 
     def m_copy(src, dst, n, to):
         return remote(mid_p.at[src], mid_p.at[dst], sem["send"], sem["m_x" if n == 0 else "m_z"], rep, to)
@@ -541,15 +541,15 @@
     with jax.named_scope("send2"):
         x = block(other, 0)
         x_first(0, x)
-        mine[1] = x[:, PART:]
+        mine_b[0] = x[:, PART:]
+    with jax.named_scope("x_far0"):
+        far(0, x_sum(0, 2))
     with jax.named_scope("relay2"):
         relay(2)
-    with jax.named_scope("x_far0"):
-        far(0, x_sum(0, 2))
+    with jax.named_scope("x_far"):
+        far(1, x_sum(1, 2))
     with jax.named_scope("relay3"):
         relay(3)
-    with jax.named_scope("x_far"):
-        far(1, x_sum(1, 2))
     with jax.named_scope("mid_x"):
         wait(mid_p.at[1], "m_x")
         mid_p[2] = (mid_p[0].astype(f32) + mid_p[1].astype(f32)).astype(bf16)
@@ -561,8 +561,8 @@
         uto[core, slot_for(t)] = ug[t, 48:80]
         o_across.start()
         x = block(a, 0)
-        mine[0] = x[:, :PART]
-        mine[2] = x[:, PART:]
+        mine_a[...] = x[:, :PART]
+        mine_b[1] = x[:, PART:]
     with jax.named_scope("relay4"):
         relay(4)
     with jax.named_scope("ou"):
@@ -577,16 +577,17 @@
         for n in range(2):
             near(n, 0, x_sum(n, 3))
     with jax.named_scope("done2"):
-        xs1[0] = (mine[1, :, :SLIM] + arrived(2)).astype(bf16)
+        xs1[0][...] = (mine_b[0, :, : WIDTHS[2]] + arrived(2)).astype(bf16)
         x1_copy(0).start()
-    with jax.named_scope("done3"):
-        xs1[1] = (mine[1, :, SLIM:] + arrived(3)).astype(bf16)
-        x1_copy(1).start()
     with jax.named_scope("x_near1"):
         for n in range(2):
             near(n, 1, x_sum(n, 1))
+    with jax.named_scope("relay00"):
+        relay(0)
+    with jax.named_scope("done3"):
+        xs1[1][...] = (mine_b[0, :, WIDTHS[2] :] + arrived(3)).astype(bf16)
+        x1_copy(1).start()
     with jax.named_scope("relay0"):
-        relay(0)
         relay(1)
     with jax.named_scope("delta"):
         wait(mid_p.at[3:6], "m_z")
@@ -595,24 +596,23 @@
             middle = middle + mid_p[n].astype(f32)
         middle = jnp.concatenate([middle, pltpu.roll(middle, 64, axis=1)], axis=0)[:, 0:64].astype(bf16)
         delta = adapter_scale * dot(middle, ou_v[...])
-        mine[0] = mine[0] + delta[:, 0:PART]
-        mine[2] = mine[2] + delta[:, PART:]
+        mine_a[...] = mine_a[...] + delta[:, 0:PART]
+        mine_b[1] = mine_b[1] + delta[:, PART:]
     with jax.named_scope("done4"):
-        mine[2] = mine[2] + arrived(4)
+        mine_b[1] = mine_b[1] + arrived(4)
     with jax.named_scope("x0_wait"):
         for n in range(2):
-            cols = slice(n * SLIM, (n + 1) * SLIM)
             x0_copy(n, 0).wait_recv()
-            mine[0, :, cols] = mine[0, :, cols] + xr0[n, 0].astype(f32)
+            mine_a[:, columns(n)] = mine_a[:, columns(n)] + xr0[n][0].astype(f32)
     with jax.named_scope("x1_wait"):
         for n in range(2):
             x1_copy(n).wait_recv()
-            cols = slice(n * SLIM, (n + 1) * SLIM)
-            out[:, PART + n * SLIM : PART + (n + 1) * SLIM] = (mine[2, :, cols] + xr1[n].astype(f32)).astype(bf16)
+            cols = columns(2 + n)
+            own = mine_b[1, :, cols.start - PART : cols.stop - PART]
+            out[:, cols] = (own + xr1[n][...].astype(f32)).astype(bf16)
     with jax.named_scope("done0"):
         for n in range(2):
-            cols = slice(n * SLIM, (n + 1) * SLIM)
-            out[:, cols] = (mine[0, :, cols] + arrived(n)).astype(bf16)
+            out[:, columns(n)] = (mine_a[:, columns(n)] + arrived(n)).astype(bf16)
 
     with jax.named_scope("drain"):
         wait(wq_v.at[0 : SENT_BYTES // 1024], "send")
@@ -659,18 +659,16 @@
             vmem((RANK, OUTC), bf16),
             vmem((QCOLS, 128), bf16),
             vmem((6, 32, 128), bf16),
-            vmem((2, 4, SEQS, SLIM), bf16),
-            vmem((2, 4, SEQS, SLIM), bf16),
-            vmem((3, 2, 32, PART), bf16),
-            vmem((3, 2, 32, PART), bf16),
-            vmem((4, 3, 2, 32, SLIM), bf16),
-            vmem((4, 3, 2, 32, SLIM), bf16),
-            vmem((2, SEQS, SLIM), bf16),
-            vmem((2, SEQS, SLIM), bf16),
-            vmem((2, 32, PART), f32),
-            vmem((4, 2, 32, SLIM), f32),
+            [vmem((4, SEQS, w), bf16) for w in WIDTHS[:2]],
+            [vmem((4, SEQS, w), bf16) for w in WIDTHS[:2]],
+            [vmem((3, 2, 32, w), bf16) for w in WIDTHS],
+            [vmem((3, 2, 32, w), bf16) for w in WIDTHS],
+            [vmem((SEQS, w), bf16) for w in WIDTHS[2:4]],
+            [vmem((SEQS, w), bf16) for w in WIDTHS[2:4]],
+            [vmem((2, 32, w), f32) for w in WIDTHS],
             vmem((4, SEQS, PART), f32),
-            vmem((3, SEQS, PART), f32),
+            vmem((SEQS, PART), f32),
+            vmem((2, SEQS, OUTC - PART), f32),
             vmem((SEQS, QCOLS), f32),
             vmem((SEQS, HEAD), f32),
             vmem((SEQS, HEAD), f32),

time: 32.5 us -> 32.4 us (level)
  no operation moved by 1% of the time
where the time goes in v6:
time: 32.4 us; the launch traced here: 32.3 us
  Pallas kernels  31.6 us (98%)
  local copies, waits for them, and re-layouts  0.66 us (2%)
    pallas_call x1, Pallas kernels, local(): pl.pallas_call(kernel, out_shape=jax.ShapeDtypeStruct((SEQS, OUTC), bf16)...  31.6 us
    unnamed x1, local copies, waits for them, and re-layouts  0.66 us

profile of v6, /device:TPU:0, one launch (start us, length us, event | category | flops | bytes accessed | tf_op | source)
XLA Modules:
  0.0 32.3 jit_solution(365002538468370106)
XLA Ops:
  0.0 31.6 %shard_map.127 = bf16[64,1024]{1,0:T(8,128)(2,1)S(1)} custom-call(bf16[64,8192]{1,0:T(8,128)(2,1)} %hidden.1, bf16[8192]{0:T(1024)(128)(2,1)} %gain.1, bf16[8192,512]{1,0:T(8,128)(2,1)} %wq.1, bf16[2,8192,128]{2,1,0:T(8,128)(2,1)} %wkv.1, bf16[512,8192]{1,0:T(8,128)(2,1)} %wo.1, bf16[3,64,64]{2,1,0:T(8,128)(2,1)} %down.1, bf16[32,64]{1,0:T(8,128)(2,1)} %bitcast.2, ...), custom_call_target="tpu_custom_call" | custom-call | flops 3000000000 | bytes 27262976 | tf_op jit(solution)/shard_map/pallas_call | solution.py:629
  31.6 0.7 %copy.15 = bf16[64,1024]{1,0:T(8,128)(2,1)} copy(bf16[64,1024]{1,0:T(8,128)(2,1)S(1)} %shard_map.127) | data formatting | bytes 262144

commit v7 on v6

--- a/solution.py
+++ b/solution.py
@@ -22,7 +22,7 @@
 OUTC = 1024
 TP = 8
 CHIPS = 8
-CHUNKS = 8
+CHUNKS = 4
 CHUNK = FEATURES // CHUNKS
 DROWS = 96
 UROWS = 80

time: 32.4 us -> 32.4 us (level)
  no operation moved by 1% of the time
where the time goes in v7:
time: 32.4 us; the launch traced here: 32.3 us
  Pallas kernels  31.6 us (98%)
  local copies, waits for them, and re-layouts  0.66 us (2%)
    pallas_call x1, Pallas kernels, local(): pl.pallas_call(kernel, out_shape=jax.ShapeDtypeStruct((SEQS, OUTC), bf16)...  31.6 us
    unnamed x1, local copies, waits for them, and re-layouts  0.66 us

profile of v7, /device:TPU:0, one launch (start us, length us, event | category | flops | bytes accessed | tf_op | source)
XLA Modules:
  0.0 32.3 jit_solution(10991732813617237763)
XLA Ops:
  0.0 31.6 %shard_map.127 = bf16[64,1024]{1,0:T(8,128)(2,1)S(1)} custom-call(bf16[64,8192]{1,0:T(8,128)(2,1)} %hidden.1, bf16[8192]{0:T(1024)(128)(2,1)} %gain.1, bf16[8192,512]{1,0:T(8,128)(2,1)} %wq.1, bf16[2,8192,128]{2,1,0:T(8,128)(2,1)} %wkv.1, bf16[512,8192]{1,0:T(8,128)(2,1)} %wo.1, bf16[3,64,64]{2,1,0:T(8,128)(2,1)} %down.1, bf16[32,64]{1,0:T(8,128)(2,1)} %bitcast.2, ...), custom_call_target="tpu_custom_call" | custom-call | flops 3000000000 | bytes 27262976 | tf_op jit(solution)/shard_map/pallas_call | solution.py:629
  31.6 0.7 %copy.15 = bf16[64,1024]{1,0:T(8,128)(2,1)} copy(bf16[64,1024]{1,0:T(8,128)(2,1)S(1)} %shard_map.127) | data formatting | bytes 262144
